TPU v7x, 1024 devices: a whole 4x8x16 slice. The times are simulated.
1024 devices in a mesh: gx: 32 (over z_hi, y), gy: 32 (over x, z_lo, core).
Axes of the slice: x: 4, y: 8, z: 16 (z_hi: 4, z_lo: 4; z = z_hi * 4 + z_lo), core: 2. Of those that a mesh axis runs over, the one named last changes fastest.
Arguments:
- checkpoint: float32 [16, 256, 4096], P(None, 'gy', 'gx'), may hold values from -6 to 6
- trajectory: float32 [16, 256, 4096], P(None, 'gy', 'gx'), may hold values from -6 to 6
- adjoint_forcing: float32 [16, 256, 4096], P(None, 'gy', 'gx'), may hold values from -6 to 6
- east_diffusion: float32 [16, 256, 4096], P(None, 'gy', 'gx'), may hold values from 0.1 to 1
- north_diffusion: float32 [16, 256, 4096], P(None, 'gy', 'gx'), may hold values from 0.3 to 3
- east_wind: float32 [16, 256, 4096], P(None, 'gy', 'gx'), may hold values from -0.6 to 0.6
- north_wind: float32 [16, 256, 4096], P(None, 'gy', 'gx'), may hold values from -6 to 6, as said below
- level_diffusion: float32 [16], replicated, may hold values from 0.1 to 1
- damping: float32 [16], replicated, may hold values from 0.2 to 2
- source: float32 [16, 256, 4096], P(None, 'gy', 'gx'), may hold values from -4 to 5
- observations: float32 [16, 256, 4096], P(None, 'gy', 'gx'), may hold values from -6 to 6
- observation_weight: float32 [16, 256, 4096], P(None, 'gy', 'gx'), may hold values from 0.1 to 1
- step_index: int32 [1], replicated, may hold values from 0 to 95
Outputs:
- forward_state: float32 [16, 256, 4096], P(None, 'gy', 'gx')
- forward_residual: float32 [16, 256, 4096], P(None, 'gy', 'gx')
- adjoint_state: float32 [16, 256, 4096], P(None, 'gy', 'gx')
Inputs may be any that keep to these rules, and one draw needn't show every extreme that they name: At every face the magnitude of north_wind is at most twice north_diffusion.
All inputs are finite; a program needn't handle non-finite values.
Results may differ from a plain program's by a relative error of at most 0.000091.
Values sent between devices are 32-bit elements; how exact they have to be, the bound alone decides.
No kernel may reach another device: no remote copies, remote signals or barrier semaphores. Data moves between devices by JAX's collectives and lax.ppermute only.
A program may use at most 32 MiB of HBM per device.

v0:
```python
import functools
import math

import jax
import jax.numpy as jnp
from jax import lax
from jax.experimental import pallas as pl
from jax.experimental.pallas import tpu as pltpu
from jax.sharding import PartitionSpec as P

DAY_STEPS = 96
RELAXATION = 0.7
SLOT = 8
FIELDS = 8
C, S, ED, EW, ND, NW, TR, AF = range(8)


def lane_ids():
    return lax.broadcasted_iota(jnp.int32, (8, 128), 1)


def turned(value, shift):
    return value if shift % 128 == 0 else pltpu.roll(value, shift % 128, 1)


def pack_kernel(size_y, x_ref, y_ref, *refs):
    fields = refs[:FIELDS]
    block, strip_odd, strip_even, far_first, far_second = refs[FIELDS:]
    odd_x, far_class, last = x_ref[0] % 2 == 1, y_ref[0] // 2 % 2 == 1, y_ref[0] == size_y - 1
    levels = fields[0].shape[0]
    half = levels // 2
    lanes = lane_ids()
    row = lax.broadcasted_iota(jnp.int32, (8, 128), 0)
    closed = jnp.where((row == 7) & last, 0.0, 1.0)
    rim_east = jnp.zeros((8, 128), jnp.float32)
    rim_west = jnp.zeros((8, 128), jnp.float32)
    for place in range(half):
        east = jnp.zeros((8, 128), jnp.float32)
        west = jnp.zeros((8, 128), jnp.float32)
        for level in (place, place + half):
            for k in range(FIELDS):
                value = fields[k][level]
                if k in (ND, NW):
                    value = value * closed
                block[k, level] = value
                base = SLOT * k + (64 if level >= half else 0)
                slot = (lanes >= base) & (lanes < base + SLOT)
                east = jnp.where(slot, turned(value, base + SLOT), east)
                west = jnp.where(slot, turned(value, base), west)
                if k == C:
                    rim_west = jnp.where(lanes == level, turned(value, level - SLOT), rim_west)
                if k in (C, ND, NW):
                    row_at = {C: 0, ND: 1, NW: 2}[k] * levels + level
                    high, low = value[7:8], value[0:1]
                    far_first[row_at : row_at + 1] = jnp.where(far_class, low, high)
                    far_second[row_at : row_at + 1] = jnp.where(far_class, high, low)
                if k in (C, ED, EW):
                    lane_at = {C: 0, ED: 1, EW: 2}[k] * levels + level
                    moved = turned(value, lane_at - (127 - SLOT))
                    rim_east = jnp.where(lanes == lane_at, moved, rim_east)
        strip_odd[place] = jnp.where(odd_x, east, west)
        strip_even[place] = jnp.where(odd_x, west, east)
    strip_odd[half] = jnp.where(odd_x, rim_east, rim_west)
    strip_even[half] = jnp.where(odd_x, rim_west, rim_east)


def corner_kernel(x_ref, from_odd, from_even, corners, rims):
    half = from_odd.shape[0] - 1
    odd_x = x_ref[0] % 2 == 1
    for place in range(half):
        corners[place] = jnp.where(odd_x, from_even[place], from_odd[place])
        corners[half + place] = jnp.where(odd_x, from_odd[place], from_even[place])
    rims[0] = jnp.where(odd_x, from_even[half], from_odd[half])
    rims[1] = jnp.where(odd_x, from_odd[half], from_even[half])


def solve_kernel(
    y_ref,
    level_ref,
    damp_ref,
    cos_ref,
    own,
    from_odd,
    from_even,
    corner_own,
    corner_odd,
    corner_even,
    rims,
    far_first,
    far_second,
    observations,
    weight,
    out_state,
    out_resid,
    out_adjoint,
    check,
    force,
    a_c,
    diag,
    up_e,
    low_w,
    up_n,
    low_s,
    low_e,
    up_w,
    low_n,
    up_s,
    wt,
    ctr,
    g,
    d,
    x,
    aq_a,
    wt_a,
    ctr_a,
    g_a,
    d_a,
    mu,
):
    levels = check.shape[0]
    lanes = lane_ids()
    rows = lax.broadcasted_iota(jnp.int32, (24, 256), 0)

    half = levels // 2
    odd_y, far_class = y_ref[0] % 2 == 1, y_ref[0] // 2 % 2 == 1

    def tile_south(k, at):
        return jnp.where(odd_y, from_even[k, at], from_odd[k, at])

    def tile_north(k, at):
        return jnp.where(odd_y, from_odd[k, at], from_even[k, at])

    def tile_own(k, at):
        return own[k, at]

    def side_south(at):
        return jnp.where(odd_y, corner_even[at], corner_odd[at])

    def side_north(at):
        return jnp.where(odd_y, corner_odd[at], corner_even[at])

    def side_own(at):
        return corner_own[at]

    def far_south(at):
        return jnp.where(far_class, far_first[at : at + 1], far_second[at : at + 1])

    def far_north(at):
        return jnp.where(far_class, far_second[at : at + 1], far_first[at : at + 1])

    def halo(k, level, west, east):
        base = SLOT * k + (64 if level >= half else 0)
        left = turned(west, 128 - SLOT - base)
        right = turned(east, -base)
        return jnp.where(lanes < SLOT, right, jnp.where(lanes >= 128 - SLOT, left, 0.0))

    def gather(k, level):
        place = level % half
        tiles = []
        for tile, strip in (
            (tile_south, side_south),
            (tile_own, side_own),
            (tile_north, side_north),
        ):
            side = halo(k, level, strip(place), strip(half + place))
            if tile is tile_own:
                if k == C:
                    side = jnp.where(lanes == SLOT, turned(rims[1], SLOT - level), side)
                if k in (C, ED, EW):
                    lane_at = {C: 0, ED: 1, EW: 2}[k] * levels + level
                    moved = turned(rims[0], 127 - SLOT - lane_at)
                    side = jnp.where(lanes == 127 - SLOT, moved, side)
            tiles.append(jnp.concatenate([tile(k, level), side], axis=1))
        return jnp.concatenate(tiles, axis=0)

    def wide(line):
        line = jnp.concatenate([line, jnp.zeros_like(line)], axis=1)
        return jnp.broadcast_to(line, (24, 256))

    def to_e(v):
        return pltpu.roll(v, 255, 1)

    def to_w(v):
        return pltpu.roll(v, 1, 1)

    def to_n(v):
        return pltpu.roll(v, 23, 0)

    def to_s(v):
        return pltpu.roll(v, 1, 0)

    def up(level):
        return level_ref[level] if level < levels - 1 else None

    def down(level):
        return level_ref[level - 1] if level > 0 else None

    def pair(level):
        parts = [u for u in (up(level), down(level)) if u is not None]
        return sum(parts[1:], parts[0])

    def with_levels(total, level, below, above):
        if above is not None:
            total = total - up(level) * above
        if below is not None:
            total = total - down(level) * below
        return total

    def forward_sum(level, v, below, above, v_n=None, v_s=None):
        v_n = to_n(v) if v_n is None else v_n
        v_s = to_s(v) if v_s is None else v_s
        total = up_e[level] * to_e(v) - low_w[level] * to_w(v)
        total = total + (up_n[level] * v_n - low_s[level] * v_s)
        return with_levels(total, level, below, above)

    def adjoint_sum(level, v, below, above):
        total = up_w[level] * to_w(v) - low_e[level] * to_e(v)
        total = total + (up_s[level] * to_s(v) - low_n[level] * to_n(v))
        return with_levels(total, level, below, above)

    def sweep(field, body):
        below, here = None, field[0]
        for level in range(levels):
            above = field[level + 1] if level + 1 < levels else None
            body(level, here, below, above)
            below, here = here, above

    for level in range(levels):
        ed = gather(ED, level)
        ew = gather(EW, level) * 0.5
        nd = gather(ND, level)
        nw = gather(NW, level) * 0.5
        far_nd = wide(far_south(levels + level))
        far_nw = wide(far_south(2 * levels + level)) * 0.5
        first = rows == 0
        e_low, e_up, n_low, n_up = ew + ed, ew - ed, nw + nd, nw - nd
        w_low, w_up = to_w(e_low), to_w(e_up)
        s_low = jnp.where(first, far_nw + far_nd, to_s(n_low))
        s_up = jnp.where(first, far_nw - far_nd, to_s(n_up))
        up_e[level] = e_up
        low_e[level] = e_low
        up_w[level] = w_up
        low_w[level] = w_low
        up_n[level] = n_up
        low_n[level] = n_low
        up_s[level] = s_up
        low_s[level] = s_low
        center = (e_low - w_up) + (n_low - s_up) + pair(level)
        a_c[level] = center
        base = ed + to_w(ed) + nd + jnp.where(first, far_nd, to_s(nd)) + (1.0 + pair(level))
        diag[level] = base
        check[level] = gather(C, level)
        force[level] = gather(S, level) * cos_ref[...]
        tangent = jnp.tanh(gather(TR, level))
        local = damp_ref[level] * (1.0 - tangent * tangent)
        weight_a = RELAXATION / (base + local)
        af = gather(AF, level)
        diagonal = 1.0 + center + local
        aq_a[level] = diagonal
        wt_a[level] = weight_a
        ctr_a[level] = 1.0 - weight_a * diagonal
        start = weight_a * af
        g_a[level] = start
        d_a[level] = start

    def newton(level, resid, tangent):
        local = damp_ref[level] * (1.0 - tangent * tangent)
        w = RELAXATION / (diag[level] + local)
        wt[level] = w
        ctr[level] = 1.0 - w * (1.0 + a_c[level] + local)
        start = -(w * resid)
        g[level] = start
        d[level] = start

    def first_resid(level, v, below, above):
        tangent = jnp.tanh(v)
        v_s = jnp.where(rows == 0, wide(far_south(level)), to_s(v))
        v_n = jnp.where(rows == 23, wide(far_north(level)), to_n(v))
        total = forward_sum(level, v, below, above, v_n, v_s)
        resid = total + a_c[level] * v + damp_ref[level] * tangent - force[level]
        newton(level, resid, tangent)

    def forward_lin(level, v, below, above):
        total = forward_sum(level, v, below, above)
        d[level] = g[level] + ctr[level] * v - wt[level] * total

    def adjoint_lin(level, v, below, above):
        total = adjoint_sum(level, v, below, above)
        d_a[level] = g_a[level] + ctr_a[level] * v - wt_a[level] * total

    def relax(field, body):
        def step(_, carry):
            sweep(field, body)
            return carry

        lax.fori_loop(0, 3, step, 0)

    sweep(check, first_resid)
    relax(d, forward_lin)

    relax(d_a, adjoint_lin)
    for level in range(levels):
        x[level] = check[level] + d[level]
        mu[level] = d_a[level]

    def second_resid(level, v, below, above):
        tangent = jnp.tanh(v)
        total = forward_sum(level, v, below, above)
        moved = v - check[level]
        resid = moved + total + a_c[level] * v + damp_ref[level] * tangent - force[level]
        newton(level, resid, tangent)

    def adjoint_resid(level, v, below, above):
        total = adjoint_sum(level, v, below, above)
        af = g_a[level]
        start = af - wt_a[level] * (total + aq_a[level] * v)
        g_a[level] = start
        d_a[level] = start

    sweep(x, second_resid)
    relax(d, forward_lin)
    sweep(mu, adjoint_resid)
    relax(d_a, adjoint_lin)
    for level in range(levels):
        final = x[level] + d[level]
        x[level] = final
        state = final[8:16, :128]
        out_state[level] = state
        multiplier = mu[level, 8:16, :128] + d_a[level, 8:16, :128]
        out_adjoint[level] = multiplier + weight[level] * (state - observations[level])

    def final_resid(level, v, below, above):
        total = forward_sum(level, v, below, above)
        moved = v - check[level]
        resid = moved + total + a_c[level] * v + damp_ref[level] * jnp.tanh(v) - force[level]
        out_resid[level] = resid[8:16, :128]

    sweep(x, final_resid)


def vmem(count):
    return [pl.BlockSpec(memory_space=pltpu.VMEM) for _ in range(count)]


def swap(array, axis, start, step, periodic):
    size = lax.axis_size(axis)
    pairs = []
    for low in range(size):
        high = low + step
        if (low - start) % (2 * step) < step and (periodic or high < size):
            pairs += [(low, high % size), (high % size, low)]
    return lax.ppermute(array, axis, pairs)


def compute(
    checkpoint,
    trajectory,
    adjoint_forcing,
    east_diffusion,
    north_diffusion,
    east_wind,
    north_wind,
    level_diffusion,
    damping,
    source,
    observations,
    observation_weight,
    step_index,
):
    levels, lat_rows, lon_cols = checkpoint.shape
    size_x = lax.axis_size("gx")
    size_y = lax.axis_size("gy")
    lane = jnp.arange(256, dtype=jnp.int32)
    column = lax.axis_index("gx") * lon_cols + lane - jnp.where(lane >= 192, 256, 0)
    column = jnp.remainder(column, lon_cols * size_x).astype(jnp.float32)
    phase = (
        2.0 * math.pi * column / (lon_cols * size_x)
        - 2.0 * math.pi * step_index[0].astype(jnp.float32) / DAY_STEPS
    )
    wave = jnp.cos(phase)[None, :]
    index_x, index_y = lax.axis_index("gx"), lax.axis_index("gy")
    place_x = index_x.astype(jnp.int32)[None]
    place_y = index_y.astype(jnp.int32)[None]
    tile = (levels, lat_rows, lon_cols)
    f32 = jnp.float32
    smem = pl.BlockSpec(memory_space=pltpu.SMEM)
    strip = (levels // 2 + 1, lat_rows, lon_cols)
    block, strip_odd, strip_even, far_a, far_b = pl.pallas_call(
        functools.partial(pack_kernel, size_y),
        in_specs=[smem, smem] + vmem(8),
        out_specs=vmem(5),
        out_shape=[
            pltpu.VMEM((FIELDS,) + tile, f32),
            pltpu.VMEM(strip, f32),
            pltpu.VMEM(strip, f32),
            pltpu.VMEM((3 * levels, lon_cols), f32),
            pltpu.VMEM((3 * levels, lon_cols), f32),
        ],
    )(
        place_x,
        place_y,
        checkpoint,
        source,
        east_diffusion,
        east_wind,
        north_diffusion,
        north_wind,
        trajectory,
        adjoint_forcing,
    )
    from_odd = swap(block, "gy", 1, 1, False)
    from_even = swap(block, "gy", 0, 1, False)
    lon_odd = swap(strip_odd, "gx", 1, 1, True)
    lon_even = swap(strip_even, "gx", 0, 1, True)
    far_first = swap(far_a, "gy", 0, 2, False)
    far_second = swap(far_b, "gy", 2, 2, False)
    corners, rims = pl.pallas_call(
        corner_kernel,
        in_specs=[smem] + vmem(2),
        out_specs=vmem(2),
        out_shape=[
            pltpu.VMEM(tile, f32),
            pltpu.VMEM((2, lat_rows, lon_cols), f32),
        ],
        compiler_params=pltpu.CompilerParams(vmem_limit_bytes=4 * 1024 * 1024),
    )(place_x, lon_odd, lon_even)
    corner_odd = swap(corners, "gy", 1, 1, False)
    corner_even = swap(corners, "gy", 0, 1, False)
    scratch = [pltpu.VMEM((levels, 24, 256), f32) for _ in range(23)]
    return tuple(
        pl.pallas_call(
            solve_kernel,
            in_specs=[smem, smem, smem] + vmem(12),
            out_specs=vmem(3),
            out_shape=[jax.ShapeDtypeStruct(tile, f32)] * 3,
            scratch_shapes=scratch,
            compiler_params=pltpu.CompilerParams(vmem_limit_bytes=20 * 1024 * 1024),
        )(
            place_y,
            level_diffusion,
            damping,
            wave,
            block,
            from_odd,
            from_even,
            corners,
            corner_odd,
            corner_even,
            rims,
            far_first,
            far_second,
            observations,
            observation_weight,
        )
    )


def solution(mesh):
    spread = P(None, "gy", "gx")
    in_specs = (spread,) * 7 + (P(), P()) + (spread,) * 3 + (P(),)
    return jax.shard_map(
        compute, mesh=mesh, in_specs=in_specs, out_specs=(spread,) * 3, check_vma=False
    )
```

profile of v0, /device:TPU:6, one launch (start us, length us, event | category | flops | bytes accessed | tf_op | source)
XLA Modules:
  0.0 63.5 jit_solution(18370249044522887049)
XLA Ops:
  0.6 0.0 copy-start.1
  0.6 1.5 %shard_map.148 = (f32[8,16,8,128]{3,2,1,0:T(8,128)S(1)}, f32[9,8,128]{2,1,0:T(8,128)S(1)}, f32[9,8,128]{2,1,0:T(8,128)S(1)}, f32[48,128]{1,0:T(8,128)S(1)}, f32[48,128]{1,0:T(8,128)S(1)}) custom-call(s32[1]{0:T(128)} %bitcast.2.x_ref, s32[1]{0:T(128)} %bitcast.y_ref, f32[16,8,128]{2,1,0:T(8,128)} %refs_0_.1, f32[16,8,128]{2,1,0:T(8,128)} %refs_1_.1, ...), custom_call_target="tpu_custom_call" | custom-call | tf_op jit(solution)/shard_map/pallas_call | solution.py:388
  2.1 0.0 copy-start
  2.2 2.1 %collective-permute-start.1 = (f32[8,16,8,128]{3,2,1,0:T(8,128)S(1)}, f32[8,16,8,128]{3,2,1,0:T(8,128)S(1)}, u32[]{:S(2)}, u32[]{:S(2)}) collective-permute-start(f32[8,16,8,128]{3,2,1,0:T(8,128)S(1)} %get-tuple-element.10.own), channel_id=1, source_target_pairs={{0,1},{1,0},{2,3},{3,2},{4,5},{5,4},{6,7},{7,6},{8,9},{9,8},{10,11... | collective-permute-start | bytes 1572872 | tf_op jit(solution)/shard_map/ppermute | solution.py:352
  4.2 8.3 %collective-permute-start = (f32[8,16,8,128]{3,2,1,0:T(8,128)S(1)}, f32[8,16,8,128]{3,2,1,0:T(8,128)S(1)}, u32[]{:S(2)}, u32[]{:S(2)}) collective-permute-start(f32[8,16,8,128]{3,2,1,0:T(8,128)S(1)} %get-tuple-element.10.own), channel_id=1, source_target_pairs={{1,2},{2,1},{3,4},{4,3},{5,6},{6,5},{7,8},{8,7},{9,10},{10,9},{11,... | collective-permute-start | bytes 1572872 | tf_op jit(solution)/shard_map/ppermute | solution.py:352
  12.5 18.4 %collective-permute-start.2 = (f32[9,8,128]{2,1,0:T(8,128)S(1)}, f32[9,8,128]{2,1,0:T(8,128)S(1)}, u32[]{:S(2)}, u32[]{:S(2)}) collective-permute-start(f32[9,8,128]{2,1,0:T(8,128)S(1)} %get-tuple-element.11), channel_id=1, source_target_pairs={{32,64},{64,32},{96,128},{128,96},{160,192},{192,160},{224,256},{2... | collective-permute-start | bytes 110600 | tf_op jit(solution)/shard_map/ppermute | solution.py:352
  30.9 1.9 %collective-permute-start.3 = (f32[9,8,128]{2,1,0:T(8,128)S(1)}, f32[9,8,128]{2,1,0:T(8,128)S(1)}, u32[]{:S(2)}, u32[]{:S(2)}) collective-permute-start(f32[9,8,128]{2,1,0:T(8,128)S(1)} %get-tuple-element.12), channel_id=1, source_target_pairs={{0,32},{32,0},{64,96},{96,64},{128,160},{160,128},{192,224},{224,1... | collective-permute-start | bytes 110600 | tf_op jit(solution)/shard_map/ppermute | solution.py:352
  32.8 1.9 %collective-permute-start.6 = (f32[48,128]{1,0:T(8,128)S(1)}, f32[48,128]{1,0:T(8,128)S(1)}, u32[]{:S(2)}, u32[]{:S(2)}) collective-permute-start(f32[48,128]{1,0:T(8,128)S(1)} %get-tuple-element.15), channel_id=1, source_target_pairs={{0,2},{2,0},{1,3},{3,1},{4,6},{6,4},{5,7},{7,5},{8,10},{10,8},{9,1... | collective-permute-start | bytes 73736 | tf_op jit(solution)/shard_map/ppermute | solution.py:352
  35.4 6.6 %collective-permute-done.2.from_odd = f32[9,8,128]{2,1,0:T(8,128)S(1)} collective-permute-done((f32[9,8,128]{2,1,0:T(8,128)S(1)}, f32[9,8,128]{2,1,0:T(8,128)S(1)}, u32[]{:S(2)}, u32[]{:S(2)}) %collective-permute-start.2) | collective-permute-done | bytes 36896 | tf_op jit(solution)/shard_map/ppermute | solution.py:352
  42.0 1.9 %collective-permute-start.7 = (f32[48,128]{1,0:T(8,128)S(1)}, f32[48,128]{1,0:T(8,128)S(1)}, u32[]{:S(2)}, u32[]{:S(2)}) collective-permute-start(f32[48,128]{1,0:T(8,128)S(1)} %get-tuple-element.16), channel_id=1, source_target_pairs={{2,4},{4,2},{3,5},{5,3},{6,8},{8,6},{7,9},{9,7},{10,12},{12,10},{1... | collective-permute-start | bytes 73736 | tf_op jit(solution)/shard_map/ppermute | solution.py:352
  43.9 0.0 collective-permute-done.3.from_even
  44.0 1.9 %collective-permute-start.5 = (f32[16,8,128]{2,1,0:T(8,128)S(1)}, f32[16,8,128]{2,1,0:T(8,128)S(1)}, u32[]{:S(2)}, u32[]{:S(2)}) collective-permute-start(f32[16,8,128]{2,1,0:T(8,128)S(1)} %get-tuple-element.13.corner_own), channel_id=1, source_target_pairs={{0,1},{1,0},{2,3},{3,2},{4,5},{5,4},{6,7},{7,6},{8,9},{9,8},{10,11... | collective-permute-start | bytes 196616 | tf_op jit(solution)/shard_map/ppermute | solution.py:352
  45.9 0.0 collective-permute-done.6.far_first
  45.9 6.7 %collective-permute-start.4 = (f32[16,8,128]{2,1,0:T(8,128)S(1)}, f32[16,8,128]{2,1,0:T(8,128)S(1)}, u32[]{:S(2)}, u32[]{:S(2)}) collective-permute-start(f32[16,8,128]{2,1,0:T(8,128)S(1)} %get-tuple-element.13.corner_own), channel_id=1, source_target_pairs={{1,2},{2,1},{3,4},{4,3},{5,6},{6,5},{7,8},{8,7},{9,10},{10,9},{11,... | collective-permute-start | bytes 196616 | tf_op jit(solution)/shard_map/ppermute | solution.py:352
  52.6 0.1 fusion.4.cos_ref
  52.7 0.0 copy-start.2
  52.7 0.0 copy-start.3
  52.7 0.0 collective-permute-done.7.far_second
  52.7 0.0 collective-permute-done.5.corner_even
  52.7 2.3 %collective-permute-done.4.corner_odd = f32[16,8,128]{2,1,0:T(8,128)S(1)} collective-permute-done((f32[16,8,128]{2,1,0:T(8,128)S(1)}, f32[16,8,128]{2,1,0:T(8,128)S(1)}, u32[]{:S(2)}, u32[]{:S(2)}) %collective-permute-start.4) | collective-permute-done | bytes 65568 | tf_op jit(solution)/shard_map/ppermute | solution.py:352
  55.1 0.0 collective-permute-done.1.from_even
  55.1 0.0 collective-permute-done.from_odd
  55.1 0.0 copy-done.1
  55.1 0.0 copy-done
  55.1 0.0 copy-done.2
  55.1 0.0 copy-done.3
  55.1 8.4 %shard_map.150 = (f32[16,8,128]{2,1,0:T(8,128)}, f32[16,8,128]{2,1,0:T(8,128)}, f32[16,8,128]{2,1,0:T(8,128)}) custom-call(s32[1]{0:T(128)} %bitcast.y_ref, f32[16]{0:T(128)S(1)} %copy-done.2, f32[16]{0:T(128)S(1)} %copy-done.3, f32[1,256]{1,0:T(1,128)S(1)} %fusion.4.cos_ref, f32[8,16,8,128]{3,2,1,0:T(8,128)S(1)} %get-tuple-element.10.own, ...), custom_call_target="tpu_custom_call" | custom-call | tf_op jit(solution)/shard_map/pallas_call | solution.py:431
  (1 shorter events, 0.0 us)
Async XLA Ops:
  0.6 54.4 %copy-start.1 = (f32[16,8,128]{2,1,0:T(8,128)S(1)}, f32[16,8,128]{2,1,0:T(8,128)}, u32[]{:S(2)}) copy-start(f32[16,8,128]{2,1,0:T(8,128)} %weight.1) | copy-start | bytes 196612
  2.1 52.9 %copy-start = (f32[16,8,128]{2,1,0:T(8,128)S(1)}, f32[16,8,128]{2,1,0:T(8,128)}, u32[]{:S(2)}) copy-start(f32[16,8,128]{2,1,0:T(8,128)} %observations.1) | copy-start | bytes 196612
  2.2 52.9 %collective-permute-start.1 = (f32[8,16,8,128]{3,2,1,0:T(8,128)S(1)}, f32[8,16,8,128]{3,2,1,0:T(8,128)S(1)}, u32[]{:S(2)}, u32[]{:S(2)}) collective-permute-start(f32[8,16,8,128]{3,2,1,0:T(8,128)S(1)} %get-tuple-element.10.own), channel_id=1, source_target_pairs={{0,1},{1,0},{2,3},{3,2},{4,5},{5,4},{6,7},{7,6},{8,9},{9,8},{10,11... | collective-permute-start | bytes 1572872 | tf_op jit(solution)/shard_map/ppermute | solution.py:352
  4.2 50.9 %collective-permute-start = (f32[8,16,8,128]{3,2,1,0:T(8,128)S(1)}, f32[8,16,8,128]{3,2,1,0:T(8,128)S(1)}, u32[]{:S(2)}, u32[]{:S(2)}) collective-permute-start(f32[8,16,8,128]{3,2,1,0:T(8,128)S(1)} %get-tuple-element.10.own), channel_id=1, source_target_pairs={{1,2},{2,1},{3,4},{4,3},{5,6},{6,5},{7,8},{8,7},{9,10},{10,9},{11,... | collective-permute-start | bytes 1572872 | tf_op jit(solution)/shard_map/ppermute | solution.py:352
  12.5 29.5 %collective-permute-start.2 = (f32[9,8,128]{2,1,0:T(8,128)S(1)}, f32[9,8,128]{2,1,0:T(8,128)S(1)}, u32[]{:S(2)}, u32[]{:S(2)}) collective-permute-start(f32[9,8,128]{2,1,0:T(8,128)S(1)} %get-tuple-element.11), channel_id=1, source_target_pairs={{32,64},{64,32},{96,128},{128,96},{160,192},{192,160},{224,256},{2... | collective-permute-start | bytes 110600 | tf_op jit(solution)/shard_map/ppermute | solution.py:352
  30.9 13.0 %collective-permute-start.3 = (f32[9,8,128]{2,1,0:T(8,128)S(1)}, f32[9,8,128]{2,1,0:T(8,128)S(1)}, u32[]{:S(2)}, u32[]{:S(2)}) collective-permute-start(f32[9,8,128]{2,1,0:T(8,128)S(1)} %get-tuple-element.12), channel_id=1, source_target_pairs={{0,32},{32,0},{64,96},{96,64},{128,160},{160,128},{192,224},{224,1... | collective-permute-start | bytes 110600 | tf_op jit(solution)/shard_map/ppermute | solution.py:352
  32.8 13.1 %collective-permute-start.6 = (f32[48,128]{1,0:T(8,128)S(1)}, f32[48,128]{1,0:T(8,128)S(1)}, u32[]{:S(2)}, u32[]{:S(2)}) collective-permute-start(f32[48,128]{1,0:T(8,128)S(1)} %get-tuple-element.15), channel_id=1, source_target_pairs={{0,2},{2,0},{1,3},{3,1},{4,6},{6,4},{5,7},{7,5},{8,10},{10,8},{9,1... | collective-permute-start | bytes 73736 | tf_op jit(solution)/shard_map/ppermute | solution.py:352
  42.0 10.7 %collective-permute-start.7 = (f32[48,128]{1,0:T(8,128)S(1)}, f32[48,128]{1,0:T(8,128)S(1)}, u32[]{:S(2)}, u32[]{:S(2)}) collective-permute-start(f32[48,128]{1,0:T(8,128)S(1)} %get-tuple-element.16), channel_id=1, source_target_pairs={{2,4},{4,2},{3,5},{5,3},{6,8},{8,6},{7,9},{9,7},{10,12},{12,10},{1... | collective-permute-start | bytes 73736 | tf_op jit(solution)/shard_map/ppermute | solution.py:352
  44.0 8.8 %collective-permute-start.5 = (f32[16,8,128]{2,1,0:T(8,128)S(1)}, f32[16,8,128]{2,1,0:T(8,128)S(1)}, u32[]{:S(2)}, u32[]{:S(2)}) collective-permute-start(f32[16,8,128]{2,1,0:T(8,128)S(1)} %get-tuple-element.13.corner_own), channel_id=1, source_target_pairs={{0,1},{1,0},{2,3},{3,2},{4,5},{5,4},{6,7},{7,6},{8,9},{9,8},{10,11... | collective-permute-start | bytes 196616 | tf_op jit(solution)/shard_map/ppermute | solution.py:352
  45.9 9.2 %collective-permute-start.4 = (f32[16,8,128]{2,1,0:T(8,128)S(1)}, f32[16,8,128]{2,1,0:T(8,128)S(1)}, u32[]{:S(2)}, u32[]{:S(2)}) collective-permute-start(f32[16,8,128]{2,1,0:T(8,128)S(1)} %get-tuple-element.13.corner_own), channel_id=1, source_target_pairs={{1,2},{2,1},{3,4},{4,3},{5,6},{6,5},{7,8},{8,7},{9,10},{10,9},{11,... | collective-permute-start | bytes 196616 | tf_op jit(solution)/shard_map/ppermute | solution.py:352
  52.7 2.4 %copy-start.2 = (f32[16]{0:T(128)S(1)}, f32[16]{0:T(128)}, u32[]{:S(2)}) copy-start(f32[16]{0:T(128)} %level_ref.1) | copy-start | bytes 196
  52.7 2.4 %copy-start.3 = (f32[16]{0:T(128)S(1)}, f32[16]{0:T(128)}, u32[]{:S(2)}) copy-start(f32[16]{0:T(128)} %damp_ref.1) | copy-start | bytes 196
where the time goes:
time: 63.9 us; the launch traced here: 63.5 us
  starting transfers between devices  43.1 us (67%)
  Pallas kernels  9.92 us (16%)
  waiting for transfers between devices  8.95 us (14%)
  between operations  1.46 us (2%)
    ppermute x8, starting transfers between devices, swap(): return lax.ppermute(array, axis, pairs)  43.1 us
    ppermute x8, waiting for transfers between devices, swap(): return lax.ppermute(array, axis, pairs)  8.95 us
    pallas_call x1, Pallas kernels, compute(): pl.pallas_call(solve_kernel, in_specs=[smem, smem, smem] + vmem(12), out_...  8.42 us
    pallas_call x1, Pallas kernels, compute(): pl.pallas_call(functools.partial(pack_kernel, size_y), in_specs=[smem, sm...  1.48 us
  transfers between devices with their start and end apart: 8, of which 2 were waited for; matrix products, arithmetic and copies ran while one was open for 0% of the time, Pallas kernels for 0%

commit v1 on v0

--- a/solution.py
+++ b/solution.py
@@ -25,8 +25,8 @@
 
 def pack_kernel(size_y, x_ref, y_ref, *refs):
     fields = refs[:FIELDS]
-    block, strip_odd, strip_even, far_first, far_second = refs[FIELDS:]
-    odd_x, far_class, last = x_ref[0] % 2 == 1, y_ref[0] // 2 % 2 == 1, y_ref[0] == size_y - 1
+    block, strip_odd, strip_even = refs[FIELDS:]
+    odd_x, last = x_ref[0] % 2 == 1, y_ref[0] == size_y - 1
     levels = fields[0].shape[0]
     half = levels // 2
     lanes = lane_ids()
@@ -49,11 +49,6 @@
                 west = jnp.where(slot, turned(value, base), west)
                 if k == C:
                     rim_west = jnp.where(lanes == level, turned(value, level - SLOT), rim_west)
-                if k in (C, ND, NW):
-                    row_at = {C: 0, ND: 1, NW: 2}[k] * levels + level
-                    high, low = value[7:8], value[0:1]
-                    far_first[row_at : row_at + 1] = jnp.where(far_class, low, high)
-                    far_second[row_at : row_at + 1] = jnp.where(far_class, high, low)
                 if k in (C, ED, EW):
                     lane_at = {C: 0, ED: 1, EW: 2}[k] * levels + level
                     moved = turned(value, lane_at - (127 - SLOT))
@@ -64,7 +59,17 @@
     strip_even[half] = jnp.where(odd_x, rim_west, rim_east)
 
 
-def corner_kernel(x_ref, from_odd, from_even, corners, rims):
+def relay(odd_y, high_when_odd, block, corners):
+    levels = block.shape[1]
+    for row in range(3 * levels):
+        value = block[(C, ND, NW)[row // levels], row % levels]
+        high, low = value[7:8], value[0:1]
+        line = jnp.where(odd_y, high, low) if high_when_odd else jnp.where(odd_y, low, high)
+        at = row % 8
+        corners[levels + row // 8, at : at + 1] = line
+
+
+def corner_odd_kernel(x_ref, y_ref, from_odd, from_even, block_even, corners, rims):
     half = from_odd.shape[0] - 1
     odd_x = x_ref[0] % 2 == 1
     for place in range(half):
@@ -72,6 +77,13 @@
         corners[half + place] = jnp.where(odd_x, from_odd[place], from_even[place])
     rims[0] = jnp.where(odd_x, from_even[half], from_odd[half])
     rims[1] = jnp.where(odd_x, from_odd[half], from_even[half])
+    relay(y_ref[0] % 2 == 1, True, block_even, corners)
+
+
+def corner_even_kernel(y_ref, corner_own, block_odd, corners):
+    for place in range(block_odd.shape[1]):
+        corners[place] = corner_own[place]
+    relay(y_ref[0] % 2 == 1, False, block_odd, corners)
 
 
 def solve_kernel(
@@ -86,8 +98,6 @@
     corner_odd,
     corner_even,
     rims,
-    far_first,
-    far_second,
     observations,
     weight,
     out_state,
@@ -122,7 +132,7 @@
     rows = lax.broadcasted_iota(jnp.int32, (24, 256), 0)
 
     half = levels // 2
-    odd_y, far_class = y_ref[0] % 2 == 1, y_ref[0] // 2 % 2 == 1
+    odd_y = y_ref[0] % 2 == 1
 
     def tile_south(k, at):
         return jnp.where(odd_y, from_even[k, at], from_odd[k, at])
@@ -143,10 +153,12 @@
         return corner_own[at]
 
     def far_south(at):
-        return jnp.where(far_class, far_first[at : at + 1], far_second[at : at + 1])
+        tile, row = levels + at // 8, at % 8
+        return side_south(tile)[row : row + 1]
 
     def far_north(at):
-        return jnp.where(far_class, far_second[at : at + 1], far_first[at : at + 1])
+        tile, row = levels + at // 8, at % 8
+        return side_north(tile)[row : row + 1]
 
     def halo(k, level, west, east):
         base = SLOT * k + (64 if level >= half else 0)
@@ -385,16 +397,14 @@
     f32 = jnp.float32
     smem = pl.BlockSpec(memory_space=pltpu.SMEM)
     strip = (levels // 2 + 1, lat_rows, lon_cols)
-    block, strip_odd, strip_even, far_a, far_b = pl.pallas_call(
+    block, strip_odd, strip_even = pl.pallas_call(
         functools.partial(pack_kernel, size_y),
         in_specs=[smem, smem] + vmem(8),
-        out_specs=vmem(5),
+        out_specs=vmem(3),
         out_shape=[
             pltpu.VMEM((FIELDS,) + tile, f32),
             pltpu.VMEM(strip, f32),
             pltpu.VMEM(strip, f32),
-            pltpu.VMEM((3 * levels, lon_cols), f32),
-            pltpu.VMEM((3 * levels, lon_cols), f32),
         ],
     )(
         place_x,
@@ -412,25 +422,32 @@
     from_even = swap(block, "gy", 0, 1, False)
     lon_odd = swap(strip_odd, "gx", 1, 1, True)
     lon_even = swap(strip_even, "gx", 0, 1, True)
-    far_first = swap(far_a, "gy", 0, 2, False)
-    far_second = swap(far_b, "gy", 2, 2, False)
+    corner_shape = (levels + 3 * levels // 8, lat_rows, lon_cols)
+    small = pltpu.CompilerParams(vmem_limit_bytes=4 * 1024 * 1024)
     corners, rims = pl.pallas_call(
-        corner_kernel,
-        in_specs=[smem] + vmem(2),
+        corner_odd_kernel,
+        in_specs=[smem, smem] + vmem(3),
         out_specs=vmem(2),
         out_shape=[
-            pltpu.VMEM(tile, f32),
+            pltpu.VMEM(corner_shape, f32),
             pltpu.VMEM((2, lat_rows, lon_cols), f32),
         ],
-        compiler_params=pltpu.CompilerParams(vmem_limit_bytes=4 * 1024 * 1024),
-    )(place_x, lon_odd, lon_even)
+        compiler_params=small,
+    )(place_x, place_y, lon_odd, lon_even, from_even)
     corner_odd = swap(corners, "gy", 1, 1, False)
-    corner_even = swap(corners, "gy", 0, 1, False)
+    corners_b = pl.pallas_call(
+        corner_even_kernel,
+        in_specs=[smem] + vmem(2),
+        out_specs=vmem(1)[0],
+        out_shape=pltpu.VMEM(corner_shape, f32),
+        compiler_params=small,
+    )(place_y, corners, from_odd)
+    corner_even = swap(corners_b, "gy", 0, 1, False)
     scratch = [pltpu.VMEM((levels, 24, 256), f32) for _ in range(23)]
     return tuple(
         pl.pallas_call(
             solve_kernel,
-            in_specs=[smem, smem, smem] + vmem(12),
+            in_specs=[smem, smem, smem] + vmem(10),
             out_specs=vmem(3),
             out_shape=[jax.ShapeDtypeStruct(tile, f32)] * 3,
             scratch_shapes=scratch,
@@ -447,8 +464,6 @@
             corner_odd,
             corner_even,
             rims,
-            far_first,
-            far_second,
             observations,
             observation_weight,
         )

time: 63.9 us -> 59.8 us (0.936)
  starting transfers between devices: 43.1 us -> 34.5 us
  waiting for transfers between devices: 8.95 us -> 13.6 us
    ppermute x8 -> x6, starting transfers between devices: 43.1 us -> 34.5 us  [swap(): return lax.ppermute(array, axis, pairs)]
    ppermute x8 -> x6, waiting for transfers between devices: 8.95 us -> 13.6 us  [swap(): return lax.ppermute(array, axis, pairs)]
    pallas_call x2 -> x3, Pallas kernels: 8.43 us -> 8.45 us  [the longest x1 8.4 us: compute(): pl.pallas_call(solve_kernel, in_specs=[smem, smem, smem] + vmem(10), out_...]
  transfers between devices with their start and end apart: 8 -> 6, of which waited for: 2 -> 2; matrix products, arithmetic and copies ran while one was open for 0% -> 0% of each run, Pallas kernels for 0% -> 0%
where the time goes in v1:
time: 59.8 us; the launch traced here: 59.5 us
  starting transfers between devices  34.5 us (58%)
  waiting for transfers between devices  13.6 us (23%)
  Pallas kernels  9.9 us (17%)
  between operations  1.42 us (2%)
    ppermute x6, starting transfers between devices, swap(): return lax.ppermute(array, axis, pairs)  34.5 us
    ppermute x6, waiting for transfers between devices, swap(): return lax.ppermute(array, axis, pairs)  13.6 us
    pallas_call x1, Pallas kernels, compute(): pl.pallas_call(solve_kernel, in_specs=[smem, smem, smem] + vmem(10), out_...  8.4 us
    pallas_call x1, Pallas kernels, compute(): pl.pallas_call(functools.partial(pack_kernel, size_y), in_specs=[smem, sm...  1.45 us
  transfers between devices with their start and end apart: 6, of which 2 were waited for; matrix products, arithmetic and copies ran while one was open for 0% of the time, Pallas kernels for 0%

profile of v1, /device:TPU:6, one launch (start us, length us, event | category | flops | bytes accessed | tf_op | source)
XLA Modules:
  0.0 59.5 jit_solution(16575060105987638964)
XLA Ops:
  0.6 1.5 %shard_map.148 = (f32[8,16,8,128]{3,2,1,0:T(8,128)S(1)}, f32[9,8,128]{2,1,0:T(8,128)S(1)}, f32[9,8,128]{2,1,0:T(8,128)S(1)}) custom-call(s32[1]{0:T(128)} %bitcast.2.x_ref, s32[1]{0:T(128)} %bitcast.y_ref, f32[16,8,128]{2,1,0:T(8,128)} %refs_0_.1, f32[16,8,128]{2,1,0:T(8,128)} %refs_1_.1, f32[16,8,128]{2,1,0:T(8,128)} %refs_2_.1, f32[16,8,128]{2,1,0:T(8,128)} %refs_3_.1, ...), custom_call_target="tpu_custom_call" | custom-call | tf_op jit(solution)/shard_map/pallas_call | solution.py:400
  2.1 1.9 %collective-permute-start.1 = (f32[8,16,8,128]{3,2,1,0:T(8,128)S(1)}, f32[8,16,8,128]{3,2,1,0:T(8,128)S(1)}, u32[]{:S(2)}, u32[]{:S(2)}) collective-permute-start(f32[8,16,8,128]{3,2,1,0:T(8,128)S(1)} %get-tuple-element.8.own), channel_id=1, source_target_pairs={{0,1},{1,0},{2,3},{3,2},{4,5},{5,4},{6,7},{7,6},{8,9},{9,8},{10,11... | collective-permute-start | bytes 1572872 | tf_op jit(solution)/shard_map/ppermute | solution.py:364
  4.0 8.3 %collective-permute-start = (f32[8,16,8,128]{3,2,1,0:T(8,128)S(1)}, f32[8,16,8,128]{3,2,1,0:T(8,128)S(1)}, u32[]{:S(2)}, u32[]{:S(2)}) collective-permute-start(f32[8,16,8,128]{3,2,1,0:T(8,128)S(1)} %get-tuple-element.8.own), channel_id=1, source_target_pairs={{1,2},{2,1},{3,4},{4,3},{5,6},{6,5},{7,8},{8,7},{9,10},{10,9},{11,... | collective-permute-start | bytes 1572872 | tf_op jit(solution)/shard_map/ppermute | solution.py:364
  12.3 18.4 %collective-permute-start.2 = (f32[9,8,128]{2,1,0:T(8,128)S(1)}, f32[9,8,128]{2,1,0:T(8,128)S(1)}, u32[]{:S(2)}, u32[]{:S(2)}) collective-permute-start(f32[9,8,128]{2,1,0:T(8,128)S(1)} %get-tuple-element.9), channel_id=1, source_target_pairs={{32,64},{64,32},{96,128},{128,96},{160,192},{192,160},{224,256},{2... | collective-permute-start | bytes 110600 | tf_op jit(solution)/shard_map/ppermute | solution.py:364
  30.7 1.9 %collective-permute-start.3 = (f32[9,8,128]{2,1,0:T(8,128)S(1)}, f32[9,8,128]{2,1,0:T(8,128)S(1)}, u32[]{:S(2)}, u32[]{:S(2)}) collective-permute-start(f32[9,8,128]{2,1,0:T(8,128)S(1)} %get-tuple-element.10), channel_id=1, source_target_pairs={{0,32},{32,0},{64,96},{96,64},{128,160},{160,128},{192,224},{224,1... | collective-permute-start | bytes 110600 | tf_op jit(solution)/shard_map/ppermute | solution.py:364
  33.3 8.3 %collective-permute-done.2.from_odd = f32[9,8,128]{2,1,0:T(8,128)S(1)} collective-permute-done((f32[9,8,128]{2,1,0:T(8,128)S(1)}, f32[9,8,128]{2,1,0:T(8,128)S(1)}, u32[]{:S(2)}, u32[]{:S(2)}) %collective-permute-start.2) | collective-permute-done | bytes 36896 | tf_op jit(solution)/shard_map/ppermute | solution.py:364
  41.5 0.0 collective-permute-done.3.from_even
  41.6 0.0 collective-permute-done.1.block_even.from_even
  41.6 0.0 copy-start
  41.6 0.0 copy-start.1
  41.6 2.1 %collective-permute-start.4 = (f32[22,8,128]{2,1,0:T(8,128)S(1)}, f32[22,8,128]{2,1,0:T(8,128)S(1)}, u32[]{:S(2)}, u32[]{:S(2)}) collective-permute-start(f32[22,8,128]{2,1,0:T(8,128)S(1)} %get-tuple-element.11.corner_own), channel_id=1, source_target_pairs={{1,2},{2,1},{3,4},{4,3},{5,6},{6,5},{7,8},{8,7},{9,10},{10,9},{11,... | collective-permute-start | bytes 270344 | tf_op jit(solution)/shard_map/ppermute | solution.py:364
  43.7 0.0 collective-permute-done.block_odd.from_odd
  43.7 1.9 %collective-permute-start.5 = (f32[22,8,128]{2,1,0:T(8,128)S(1)}, f32[22,8,128]{2,1,0:T(8,128)S(1)}, u32[]{:S(2)}, u32[]{:S(2)}) collective-permute-start(f32[22,8,128]{2,1,0:T(8,128)S(1)} %shard_map.150), channel_id=1, source_target_pairs={{0,1},{1,0},{2,3},{3,2},{4,5},{5,4},{6,7},{7,6},{8,9},{9,8},{10,11... | collective-permute-start | bytes 270344 | tf_op jit(solution)/shard_map/ppermute | solution.py:364
  45.6 0.1 fusion.4.cos_ref
  45.7 0.0 copy-start.2
  45.7 0.0 copy-start.3
  45.7 5.3 %collective-permute-done.4.corner_odd = f32[22,8,128]{2,1,0:T(8,128)S(1)} collective-permute-done((f32[22,8,128]{2,1,0:T(8,128)S(1)}, f32[22,8,128]{2,1,0:T(8,128)S(1)}, u32[]{:S(2)}, u32[]{:S(2)}) %collective-permute-start.4) | collective-permute-done | bytes 90144 | tf_op jit(solution)/shard_map/ppermute | solution.py:364
  51.1 0.0 collective-permute-done.5.corner_even
  51.1 0.0 copy-done
  51.1 0.0 copy-done.1
  51.1 0.0 copy-done.2
  51.1 0.0 copy-done.3
  51.1 8.4 %shard_map.151 = (f32[16,8,128]{2,1,0:T(8,128)}, f32[16,8,128]{2,1,0:T(8,128)}, f32[16,8,128]{2,1,0:T(8,128)}) custom-call(s32[1]{0:T(128)} %bitcast.y_ref, f32[16]{0:T(128)S(1)} %copy-done.2, f32[16]{0:T(128)S(1)} %copy-done.3, f32[1,256]{1,0:T(1,128)S(1)} %fusion.4.cos_ref, f32[8,16,8,128]{3,2,1,0:T(8,128)S(1)} %get-tuple-element.8.own, ...), custom_call_target="tpu_custom_call" | custom-call | tf_op jit(solution)/shard_map/pallas_call | solution.py:448
  (2 shorter events, 0.1 us)
Async XLA Ops:
  2.1 39.5 %collective-permute-start.1 = (f32[8,16,8,128]{3,2,1,0:T(8,128)S(1)}, f32[8,16,8,128]{3,2,1,0:T(8,128)S(1)}, u32[]{:S(2)}, u32[]{:S(2)}) collective-permute-start(f32[8,16,8,128]{3,2,1,0:T(8,128)S(1)} %get-tuple-element.8.own), channel_id=1, source_target_pairs={{0,1},{1,0},{2,3},{3,2},{4,5},{5,4},{6,7},{7,6},{8,9},{9,8},{10,11... | collective-permute-start | bytes 1572872 | tf_op jit(solution)/shard_map/ppermute | solution.py:364
  4.0 39.6 %collective-permute-start = (f32[8,16,8,128]{3,2,1,0:T(8,128)S(1)}, f32[8,16,8,128]{3,2,1,0:T(8,128)S(1)}, u32[]{:S(2)}, u32[]{:S(2)}) collective-permute-start(f32[8,16,8,128]{3,2,1,0:T(8,128)S(1)} %get-tuple-element.8.own), channel_id=1, source_target_pairs={{1,2},{2,1},{3,4},{4,3},{5,6},{6,5},{7,8},{8,7},{9,10},{10,9},{11,... | collective-permute-start | bytes 1572872 | tf_op jit(solution)/shard_map/ppermute | solution.py:364
  12.3 29.3 %collective-permute-start.2 = (f32[9,8,128]{2,1,0:T(8,128)S(1)}, f32[9,8,128]{2,1,0:T(8,128)S(1)}, u32[]{:S(2)}, u32[]{:S(2)}) collective-permute-start(f32[9,8,128]{2,1,0:T(8,128)S(1)} %get-tuple-element.9), channel_id=1, source_target_pairs={{32,64},{64,32},{96,128},{128,96},{160,192},{192,160},{224,256},{2... | collective-permute-start | bytes 110600 | tf_op jit(solution)/shard_map/ppermute | solution.py:364
  30.7 10.8 %collective-permute-start.3 = (f32[9,8,128]{2,1,0:T(8,128)S(1)}, f32[9,8,128]{2,1,0:T(8,128)S(1)}, u32[]{:S(2)}, u32[]{:S(2)}) collective-permute-start(f32[9,8,128]{2,1,0:T(8,128)S(1)} %get-tuple-element.10), channel_id=1, source_target_pairs={{0,32},{32,0},{64,96},{96,64},{128,160},{160,128},{192,224},{224,1... | collective-permute-start | bytes 110600 | tf_op jit(solution)/shard_map/ppermute | solution.py:364
  41.6 9.5 %copy-start = (f32[16,8,128]{2,1,0:T(8,128)S(1)}, f32[16,8,128]{2,1,0:T(8,128)}, u32[]{:S(2)}) copy-start(f32[16,8,128]{2,1,0:T(8,128)} %observations.1) | copy-start | bytes 196612
  41.6 9.5 %copy-start.1 = (f32[16,8,128]{2,1,0:T(8,128)S(1)}, f32[16,8,128]{2,1,0:T(8,128)}, u32[]{:S(2)}) copy-start(f32[16,8,128]{2,1,0:T(8,128)} %weight.1) | copy-start | bytes 196612
  41.6 9.4 %collective-permute-start.4 = (f32[22,8,128]{2,1,0:T(8,128)S(1)}, f32[22,8,128]{2,1,0:T(8,128)S(1)}, u32[]{:S(2)}, u32[]{:S(2)}) collective-permute-start(f32[22,8,128]{2,1,0:T(8,128)S(1)} %get-tuple-element.11.corner_own), channel_id=1, source_target_pairs={{1,2},{2,1},{3,4},{4,3},{5,6},{6,5},{7,8},{8,7},{9,10},{10,9},{11,... | collective-permute-start | bytes 270344 | tf_op jit(solution)/shard_map/ppermute | solution.py:364
  43.7 7.3 %collective-permute-start.5 = (f32[22,8,128]{2,1,0:T(8,128)S(1)}, f32[22,8,128]{2,1,0:T(8,128)S(1)}, u32[]{:S(2)}, u32[]{:S(2)}) collective-permute-start(f32[22,8,128]{2,1,0:T(8,128)S(1)} %shard_map.150), channel_id=1, source_target_pairs={{0,1},{1,0},{2,3},{3,2},{4,5},{5,4},{6,7},{7,6},{8,9},{9,8},{10,11... | collective-permute-start | bytes 270344 | tf_op jit(solution)/shard_map/ppermute | solution.py:364
  45.7 5.4 %copy-start.2 = (f32[16]{0:T(128)S(1)}, f32[16]{0:T(128)}, u32[]{:S(2)}) copy-start(f32[16]{0:T(128)} %level_ref.1) | copy-start | bytes 196
  45.7 5.4 %copy-start.3 = (f32[16]{0:T(128)S(1)}, f32[16]{0:T(128)}, u32[]{:S(2)}) copy-start(f32[16]{0:T(128)} %damp_ref.1) | copy-start | bytes 196

commit v2 on v1

--- a/solution.py
+++ b/solution.py
@@ -12,6 +12,7 @@
 RELAXATION = 0.7
 SLOT = 8
 FIELDS = 8
+FORWARD = 6
 C, S, ED, EW, ND, NW, TR, AF = range(8)
 
 
@@ -25,7 +26,7 @@
 
 def pack_kernel(size_y, x_ref, y_ref, *refs):
     fields = refs[:FIELDS]
-    block, strip_odd, strip_even = refs[FIELDS:]
+    block, block_f, strip_odd, strip_even = refs[FIELDS:]
     odd_x, last = x_ref[0] % 2 == 1, y_ref[0] == size_y - 1
     levels = fields[0].shape[0]
     half = levels // 2
@@ -43,6 +44,8 @@
                 if k in (ND, NW):
                     value = value * closed
                 block[k, level] = value
+                if k < FORWARD:
+                    block_f[k, level] = value
                 base = SLOT * k + (64 if level >= half else 0)
                 slot = (lanes >= base) & (lanes < base + SLOT)
                 east = jnp.where(slot, turned(value, base + SLOT), east)
@@ -69,7 +72,7 @@
         corners[levels + row // 8, at : at + 1] = line
 
 
-def corner_odd_kernel(x_ref, y_ref, from_odd, from_even, block_even, corners, rims):
+def corner_odd_kernel(x_ref, y_ref, from_odd, from_even, block_even, block, corners, rims):
     half = from_odd.shape[0] - 1
     odd_x = x_ref[0] % 2 == 1
     for place in range(half):
@@ -78,6 +81,11 @@
     rims[0] = jnp.where(odd_x, from_even[half], from_odd[half])
     rims[1] = jnp.where(odd_x, from_odd[half], from_even[half])
     relay(y_ref[0] % 2 == 1, True, block_even, corners)
+    levels = block.shape[1]
+    base = levels + 3 * levels // 8
+    for k in range(FORWARD, FIELDS):
+        for level in range(levels):
+            corners[base + (k - FORWARD) * levels + level] = block[k, level]
 
 
 def corner_even_kernel(y_ref, corner_own, block_odd, corners):
@@ -134,11 +142,16 @@
     half = levels // 2
     odd_y = y_ref[0] % 2 == 1
 
+    def odd_tile(k, at):
+        if k < FORWARD:
+            return from_odd[k, at]
+        return corner_odd[levels + 3 * levels // 8 + (k - FORWARD) * levels + at]
+
     def tile_south(k, at):
-        return jnp.where(odd_y, from_even[k, at], from_odd[k, at])
+        return jnp.where(odd_y, from_even[k, at], odd_tile(k, at))
 
     def tile_north(k, at):
-        return jnp.where(odd_y, from_odd[k, at], from_even[k, at])
+        return jnp.where(odd_y, odd_tile(k, at), from_even[k, at])
 
     def tile_own(k, at):
         return own[k, at]
@@ -397,12 +410,13 @@
     f32 = jnp.float32
     smem = pl.BlockSpec(memory_space=pltpu.SMEM)
     strip = (levels // 2 + 1, lat_rows, lon_cols)
-    block, strip_odd, strip_even = pl.pallas_call(
+    block, block_f, strip_odd, strip_even = pl.pallas_call(
         functools.partial(pack_kernel, size_y),
         in_specs=[smem, smem] + vmem(8),
-        out_specs=vmem(3),
+        out_specs=vmem(4),
         out_shape=[
             pltpu.VMEM((FIELDS,) + tile, f32),
+            pltpu.VMEM((FORWARD,) + tile, f32),
             pltpu.VMEM(strip, f32),
             pltpu.VMEM(strip, f32),
         ],
@@ -418,7 +432,7 @@
         trajectory,
         adjoint_forcing,
     )
-    from_odd = swap(block, "gy", 1, 1, False)
+    from_odd = swap(block_f, "gy", 1, 1, False)
     from_even = swap(block, "gy", 0, 1, False)
     lon_odd = swap(strip_odd, "gx", 1, 1, True)
     lon_even = swap(strip_even, "gx", 0, 1, True)
@@ -426,14 +440,14 @@
     small = pltpu.CompilerParams(vmem_limit_bytes=4 * 1024 * 1024)
     corners, rims = pl.pallas_call(
         corner_odd_kernel,
-        in_specs=[smem, smem] + vmem(3),
+        in_specs=[smem, smem] + vmem(4),
         out_specs=vmem(2),
         out_shape=[
-            pltpu.VMEM(corner_shape, f32),
+            pltpu.VMEM((corner_shape[0] + 2 * levels,) + corner_shape[1:], f32),
             pltpu.VMEM((2, lat_rows, lon_cols), f32),
         ],
         compiler_params=small,
-    )(place_x, place_y, lon_odd, lon_even, from_even)
+    )(place_x, place_y, lon_odd, lon_even, from_even, block)
     corner_odd = swap(corners, "gy", 1, 1, False)
     corners_b = pl.pallas_call(
         corner_even_kernel,

time: 59.8 us -> 59.4 us (level)
  waiting for transfers between devices: 13.6 us -> 12.9 us
    ppermute x6, waiting for transfers between devices: 13.6 us -> 12.9 us  [swap(): return lax.ppermute(array, axis, pairs)]
  transfers between devices with their start and end apart: 6 -> 6, of which waited for: 2 -> 3; matrix products, arithmetic and copies ran while one was open for 0% -> 0% of each run, Pallas kernels for 0% -> 0%
where the time goes in v2:
time: 59.4 us; the launch traced here: 58.7 us
  starting transfers between devices  34.3 us (58%)
  waiting for transfers between devices  12.9 us (22%)
  Pallas kernels  9.92 us (17%)
  between operations  1.41 us (2%)
    ppermute x6, starting transfers between devices, swap(): return lax.ppermute(array, axis, pairs)  34.3 us
    ppermute x6, waiting for transfers between devices, swap(): return lax.ppermute(array, axis, pairs)  12.9 us
    pallas_call x1, Pallas kernels, compute(): pl.pallas_call(solve_kernel, in_specs=[smem, smem, smem] + vmem(10), out_...  8.4 us
    pallas_call x1, Pallas kernels, compute(): pl.pallas_call(functools.partial(pack_kernel, size_y), in_specs=[smem, sm...  1.45 us
  transfers between devices with their start and end apart: 6, of which 3 were waited for; matrix products, arithmetic and copies ran while one was open for 0% of the time, Pallas kernels for 0%

profile of v2, /device:TPU:6, one launch (start us, length us, event | category | flops | bytes accessed | tf_op | source)
XLA Modules:
  0.0 58.7 jit_solution(17951883249620387592)
XLA Ops:
  0.6 1.4 %shard_map.148 = (f32[8,16,8,128]{3,2,1,0:T(8,128)S(1)}, f32[6,16,8,128]{3,2,1,0:T(8,128)S(1)}, f32[9,8,128]{2,1,0:T(8,128)S(1)}, f32[9,8,128]{2,1,0:T(8,128)S(1)}) custom-call(s32[1]{0:T(128)} %bitcast.2.x_ref, s32[1]{0:T(128)} %bitcast.y_ref, f32[16,8,128]{2,1,0:T(8,128)} %refs_0_.1, f32[16,8,128]{2,1,0:T(8,128)} %refs_1_.1, f32[16,8,128]{2,1,0:T(8,128)} %refs_2_.1, ...), custom_call_target="tpu_custom_call" | custom-call | tf_op jit(solution)/shard_map/pallas_call | solution.py:413
  2.1 1.9 %collective-permute-start.1 = (f32[8,16,8,128]{3,2,1,0:T(8,128)S(1)}, f32[8,16,8,128]{3,2,1,0:T(8,128)S(1)}, u32[]{:S(2)}, u32[]{:S(2)}) collective-permute-start(f32[8,16,8,128]{3,2,1,0:T(8,128)S(1)} %get-tuple-element.9.block.own), channel_id=1, source_target_pairs={{0,1},{1,0},{2,3},{3,2},{4,5},{5,4},{6,7},{7,6},{8,9},{9,8},{10,11... | collective-permute-start | bytes 1572872 | tf_op jit(solution)/shard_map/ppermute | solution.py:377
  4.0 8.3 %collective-permute-start = (f32[6,16,8,128]{3,2,1,0:T(8,128)S(1)}, f32[6,16,8,128]{3,2,1,0:T(8,128)S(1)}, u32[]{:S(2)}, u32[]{:S(2)}) collective-permute-start(f32[6,16,8,128]{3,2,1,0:T(8,128)S(1)} %get-tuple-element.10), channel_id=1, source_target_pairs={{1,2},{2,1},{3,4},{4,3},{5,6},{6,5},{7,8},{8,7},{9,10},{10,9},{11,... | collective-permute-start | bytes 1179656 | tf_op jit(solution)/shard_map/ppermute | solution.py:377
  12.3 18.4 %collective-permute-start.2 = (f32[9,8,128]{2,1,0:T(8,128)S(1)}, f32[9,8,128]{2,1,0:T(8,128)S(1)}, u32[]{:S(2)}, u32[]{:S(2)}) collective-permute-start(f32[9,8,128]{2,1,0:T(8,128)S(1)} %get-tuple-element.11), channel_id=1, source_target_pairs={{32,64},{64,32},{96,128},{128,96},{160,192},{192,160},{224,256},{2... | collective-permute-start | bytes 110600 | tf_op jit(solution)/shard_map/ppermute | solution.py:377
  30.7 1.9 %collective-permute-start.3 = (f32[9,8,128]{2,1,0:T(8,128)S(1)}, f32[9,8,128]{2,1,0:T(8,128)S(1)}, u32[]{:S(2)}, u32[]{:S(2)}) collective-permute-start(f32[9,8,128]{2,1,0:T(8,128)S(1)} %get-tuple-element.12), channel_id=1, source_target_pairs={{0,32},{32,0},{64,96},{96,64},{128,160},{160,128},{192,224},{224,1... | collective-permute-start | bytes 110600 | tf_op jit(solution)/shard_map/ppermute | solution.py:377
  32.6 5.6 %collective-permute-done.2.from_odd = f32[9,8,128]{2,1,0:T(8,128)S(1)} collective-permute-done((f32[9,8,128]{2,1,0:T(8,128)S(1)}, f32[9,8,128]{2,1,0:T(8,128)S(1)}, u32[]{:S(2)}, u32[]{:S(2)}) %collective-permute-start.2) | collective-permute-done | bytes 36896 | tf_op jit(solution)/shard_map/ppermute | solution.py:377
  38.2 0.0 collective-permute-done.3.from_even
  38.2 0.0 collective-permute-done.1.block_even.from_even
  38.3 1.9 %collective-permute-start.4 = (f32[54,8,128]{2,1,0:T(8,128)S(1)}, f32[54,8,128]{2,1,0:T(8,128)S(1)}, u32[]{:S(2)}, u32[]{:S(2)}) collective-permute-start(f32[54,8,128]{2,1,0:T(8,128)S(1)} %get-tuple-element.13.corner_own), channel_id=1, source_target_pairs={{1,2},{2,1},{3,4},{4,3},{5,6},{6,5},{7,8},{8,7},{9,10},{10,9},{11,... | collective-permute-start | bytes 663560 | tf_op jit(solution)/shard_map/ppermute | solution.py:377
  40.8 0.0 copy-start
  40.9 0.0 copy-start.1
  40.9 0.0 collective-permute-done.block_odd.from_odd
  40.9 1.9 %collective-permute-start.5 = (f32[22,8,128]{2,1,0:T(8,128)S(1)}, f32[22,8,128]{2,1,0:T(8,128)S(1)}, u32[]{:S(2)}, u32[]{:S(2)}) collective-permute-start(f32[22,8,128]{2,1,0:T(8,128)S(1)} %shard_map.150), channel_id=1, source_target_pairs={{0,1},{1,0},{2,3},{3,2},{4,5},{5,4},{6,7},{7,6},{8,9},{9,8},{10,11... | collective-permute-start | bytes 270344 | tf_op jit(solution)/shard_map/ppermute | solution.py:377
  42.8 0.1 fusion.4.cos_ref
  42.9 0.0 copy-start.2
  42.9 0.0 copy-start.3
  42.9 1.2 %collective-permute-done.5.corner_even = f32[22,8,128]{2,1,0:T(8,128)S(1)} collective-permute-done((f32[22,8,128]{2,1,0:T(8,128)S(1)}, f32[22,8,128]{2,1,0:T(8,128)S(1)}, u32[]{:S(2)}, u32[]{:S(2)}) %collective-permute-start.5) | collective-permute-done | bytes 90144 | tf_op jit(solution)/shard_map/ppermute | solution.py:377
  44.1 6.2 %collective-permute-done.4.corner_odd = f32[54,8,128]{2,1,0:T(8,128)S(1)} collective-permute-done((f32[54,8,128]{2,1,0:T(8,128)S(1)}, f32[54,8,128]{2,1,0:T(8,128)S(1)}, u32[]{:S(2)}, u32[]{:S(2)}) %collective-permute-start.4) | collective-permute-done | bytes 221216 | tf_op jit(solution)/shard_map/ppermute | solution.py:377
  50.3 0.0 copy-done
  50.3 0.0 copy-done.1
  50.3 0.0 copy-done.2
  50.3 0.0 copy-done.3
  50.3 8.4 %shard_map.151 = (f32[16,8,128]{2,1,0:T(8,128)}, f32[16,8,128]{2,1,0:T(8,128)}, f32[16,8,128]{2,1,0:T(8,128)}) custom-call(s32[1]{0:T(128)} %bitcast.y_ref, f32[16]{0:T(128)S(1)} %copy-done.2, f32[16]{0:T(128)S(1)} %copy-done.3, f32[1,256]{1,0:T(1,128)S(1)} %fusion.4.cos_ref, f32[8,16,8,128]{3,2,1,0:T(8,128)S(1)} %get-tuple-element.9.block.own, ...), custom_call_target="tpu_custom_call" | custom-call | tf_op jit(solution)/shard_map/pallas_call | solution.py:462
  (2 shorter events, 0.1 us)
Async XLA Ops:
  2.1 36.1 %collective-permute-start.1 = (f32[8,16,8,128]{3,2,1,0:T(8,128)S(1)}, f32[8,16,8,128]{3,2,1,0:T(8,128)S(1)}, u32[]{:S(2)}, u32[]{:S(2)}) collective-permute-start(f32[8,16,8,128]{3,2,1,0:T(8,128)S(1)} %get-tuple-element.9.block.own), channel_id=1, source_target_pairs={{0,1},{1,0},{2,3},{3,2},{4,5},{5,4},{6,7},{7,6},{8,9},{9,8},{10,11... | collective-permute-start | bytes 1572872 | tf_op jit(solution)/shard_map/ppermute | solution.py:377
  4.0 36.8 %collective-permute-start = (f32[6,16,8,128]{3,2,1,0:T(8,128)S(1)}, f32[6,16,8,128]{3,2,1,0:T(8,128)S(1)}, u32[]{:S(2)}, u32[]{:S(2)}) collective-permute-start(f32[6,16,8,128]{3,2,1,0:T(8,128)S(1)} %get-tuple-element.10), channel_id=1, source_target_pairs={{1,2},{2,1},{3,4},{4,3},{5,6},{6,5},{7,8},{8,7},{9,10},{10,9},{11,... | collective-permute-start | bytes 1179656 | tf_op jit(solution)/shard_map/ppermute | solution.py:377
  12.3 25.9 %collective-permute-start.2 = (f32[9,8,128]{2,1,0:T(8,128)S(1)}, f32[9,8,128]{2,1,0:T(8,128)S(1)}, u32[]{:S(2)}, u32[]{:S(2)}) collective-permute-start(f32[9,8,128]{2,1,0:T(8,128)S(1)} %get-tuple-element.11), channel_id=1, source_target_pairs={{32,64},{64,32},{96,128},{128,96},{160,192},{192,160},{224,256},{2... | collective-permute-start | bytes 110600 | tf_op jit(solution)/shard_map/ppermute | solution.py:377
  30.7 7.5 %collective-permute-start.3 = (f32[9,8,128]{2,1,0:T(8,128)S(1)}, f32[9,8,128]{2,1,0:T(8,128)S(1)}, u32[]{:S(2)}, u32[]{:S(2)}) collective-permute-start(f32[9,8,128]{2,1,0:T(8,128)S(1)} %get-tuple-element.12), channel_id=1, source_target_pairs={{0,32},{32,0},{64,96},{96,64},{128,160},{160,128},{192,224},{224,1... | collective-permute-start | bytes 110600 | tf_op jit(solution)/shard_map/ppermute | solution.py:377
  38.3 12.0 %collective-permute-start.4 = (f32[54,8,128]{2,1,0:T(8,128)S(1)}, f32[54,8,128]{2,1,0:T(8,128)S(1)}, u32[]{:S(2)}, u32[]{:S(2)}) collective-permute-start(f32[54,8,128]{2,1,0:T(8,128)S(1)} %get-tuple-element.13.corner_own), channel_id=1, source_target_pairs={{1,2},{2,1},{3,4},{4,3},{5,6},{6,5},{7,8},{8,7},{9,10},{10,9},{11,... | collective-permute-start | bytes 663560 | tf_op jit(solution)/shard_map/ppermute | solution.py:377
  40.8 9.4 %copy-start = (f32[16,8,128]{2,1,0:T(8,128)S(1)}, f32[16,8,128]{2,1,0:T(8,128)}, u32[]{:S(2)}) copy-start(f32[16,8,128]{2,1,0:T(8,128)} %observations.1) | copy-start | bytes 196612
  40.9 9.4 %copy-start.1 = (f32[16,8,128]{2,1,0:T(8,128)S(1)}, f32[16,8,128]{2,1,0:T(8,128)}, u32[]{:S(2)}) copy-start(f32[16,8,128]{2,1,0:T(8,128)} %weight.1) | copy-start | bytes 196612
  40.9 3.2 %collective-permute-start.5 = (f32[22,8,128]{2,1,0:T(8,128)S(1)}, f32[22,8,128]{2,1,0:T(8,128)S(1)}, u32[]{:S(2)}, u32[]{:S(2)}) collective-permute-start(f32[22,8,128]{2,1,0:T(8,128)S(1)} %shard_map.150), channel_id=1, source_target_pairs={{0,1},{1,0},{2,3},{3,2},{4,5},{5,4},{6,7},{7,6},{8,9},{9,8},{10,11... | collective-permute-start | bytes 270344 | tf_op jit(solution)/shard_map/ppermute | solution.py:377
  42.9 7.4 %copy-start.2 = (f32[16]{0:T(128)S(1)}, f32[16]{0:T(128)}, u32[]{:S(2)}) copy-start(f32[16]{0:T(128)} %level_ref.1) | copy-start | bytes 196
  42.9 7.4 %copy-start.3 = (f32[16]{0:T(128)S(1)}, f32[16]{0:T(128)}, u32[]{:S(2)}) copy-start(f32[16]{0:T(128)} %damp_ref.1) | copy-start | bytes 196

commit v3 on v1

--- a/solution.py
+++ b/solution.py
@@ -12,6 +12,7 @@
 RELAXATION = 0.7
 SLOT = 8
 FIELDS = 8
+FORWARD = 6
 C, S, ED, EW, ND, NW, TR, AF = range(8)
 
 
@@ -25,7 +26,7 @@
 
 def pack_kernel(size_y, x_ref, y_ref, *refs):
     fields = refs[:FIELDS]
-    block, strip_odd, strip_even = refs[FIELDS:]
+    block, block_f, block_a, strip_odd, strip_even = refs[FIELDS:]
     odd_x, last = x_ref[0] % 2 == 1, y_ref[0] == size_y - 1
     levels = fields[0].shape[0]
     half = levels // 2
@@ -43,6 +44,10 @@
                 if k in (ND, NW):
                     value = value * closed
                 block[k, level] = value
+                if k < FORWARD:
+                    block_f[k, level] = value
+                else:
+                    block_a[k - FORWARD, level] = value
                 base = SLOT * k + (64 if level >= half else 0)
                 slot = (lanes >= base) & (lanes < base + SLOT)
                 east = jnp.where(slot, turned(value, base + SLOT), east)
@@ -86,59 +91,32 @@
     relay(y_ref[0] % 2 == 1, False, block_odd, corners)
 
 
-def solve_kernel(
-    y_ref,
-    level_ref,
-    damp_ref,
-    cos_ref,
-    own,
-    from_odd,
-    from_even,
-    corner_own,
-    corner_odd,
-    corner_even,
-    rims,
-    observations,
-    weight,
-    out_state,
-    out_resid,
-    out_adjoint,
-    check,
-    force,
-    a_c,
-    diag,
-    up_e,
-    low_w,
-    up_n,
-    low_s,
-    low_e,
-    up_w,
-    low_n,
-    up_s,
-    wt,
-    ctr,
-    g,
-    d,
-    x,
-    aq_a,
-    wt_a,
-    ctr_a,
-    g_a,
-    d_a,
-    mu,
-):
-    levels = check.shape[0]
+def turn_e(v):
+    return pltpu.roll(v, 255, 1)
+
+
+def turn_w(v):
+    return pltpu.roll(v, 1, 1)
+
+
+def turn_n(v):
+    return pltpu.roll(v, 23, 0)
+
+
+def turn_s(v):
+    return pltpu.roll(v, 1, 0)
+
+
+def gatherer(odd_y, own, odd_tile, from_even, corner_own, corner_odd, corner_even, rims):
+    levels = own.shape[1]
+    half = levels // 2
     lanes = lane_ids()
-    rows = lax.broadcasted_iota(jnp.int32, (24, 256), 0)
-
-    half = levels // 2
-    odd_y = y_ref[0] % 2 == 1
 
     def tile_south(k, at):
-        return jnp.where(odd_y, from_even[k, at], from_odd[k, at])
+        return jnp.where(odd_y, from_even[k, at], odd_tile(k, at))
 
     def tile_north(k, at):
-        return jnp.where(odd_y, from_odd[k, at], from_even[k, at])
+        return jnp.where(odd_y, odd_tile(k, at), from_even[k, at])
 
     def tile_own(k, at):
         return own[k, at]
@@ -185,57 +163,99 @@
             tiles.append(jnp.concatenate([tile(k, level), side], axis=1))
         return jnp.concatenate(tiles, axis=0)
 
+    return gather, far_south, far_north
+
+
+def level_pair(level_ref, level, levels):
+    parts = []
+    if level < levels - 1:
+        parts.append(level_ref[level])
+    if level > 0:
+        parts.append(level_ref[level - 1])
+    return sum(parts[1:], parts[0])
+
+
+def with_levels(level_ref, total, level, below, above):
+    if above is not None:
+        total = total - level_ref[level] * above
+    if below is not None:
+        total = total - level_ref[level - 1] * below
+    return total
+
+
+def sweep(field, body):
+    levels = field.shape[0]
+    below, here = None, field[0]
+    for level in range(levels):
+        above = field[level + 1] if level + 1 < levels else None
+        body(level, here, below, above)
+        below, here = here, above
+
+
+def relax(field, body):
+    def step(_, carry):
+        sweep(field, body)
+        return carry
+
+    lax.fori_loop(0, 3, step, 0)
+
+
+def forward_kernel(
+    y_ref,
+    level_ref,
+    damp_ref,
+    cos_ref,
+    own,
+    from_odd,
+    from_even,
+    corner_own,
+    corner_odd,
+    corner_even,
+    rims,
+    out_state,
+    out_resid,
+    keep_state,
+    a_c,
+    diag,
+    low_e,
+    up_w,
+    low_n,
+    up_s,
+    check,
+    force,
+    up_e,
+    low_w,
+    up_n,
+    low_s,
+    wt,
+    ctr,
+    g,
+    d,
+    x,
+):
+    levels = check.shape[0]
+    rows = lax.broadcasted_iota(jnp.int32, (24, 256), 0)
+    gather, far_south, far_north = gatherer(
+        y_ref[0] % 2 == 1,
+        own,
+        lambda k, at: from_odd[k, at],
+        from_even,
+        corner_own,
+        corner_odd,
+        corner_even,
+        rims,
+    )
+
     def wide(line):
         line = jnp.concatenate([line, jnp.zeros_like(line)], axis=1)
         return jnp.broadcast_to(line, (24, 256))
 
-    def to_e(v):
-        return pltpu.roll(v, 255, 1)
-
-    def to_w(v):
-        return pltpu.roll(v, 1, 1)
-
-    def to_n(v):
-        return pltpu.roll(v, 23, 0)
-
-    def to_s(v):
-        return pltpu.roll(v, 1, 0)
-
-    def up(level):
-        return level_ref[level] if level < levels - 1 else None
-
-    def down(level):
-        return level_ref[level - 1] if level > 0 else None
-
-    def pair(level):
-        parts = [u for u in (up(level), down(level)) if u is not None]
-        return sum(parts[1:], parts[0])
-
-    def with_levels(total, level, below, above):
-        if above is not None:
-            total = total - up(level) * above
-        if below is not None:
-            total = total - down(level) * below
-        return total
-
     def forward_sum(level, v, below, above, v_n=None, v_s=None):
-        v_n = to_n(v) if v_n is None else v_n
-        v_s = to_s(v) if v_s is None else v_s
-        total = up_e[level] * to_e(v) - low_w[level] * to_w(v)
+        v_n = turn_n(v) if v_n is None else v_n
+        v_s = turn_s(v) if v_s is None else v_s
+        total = up_e[level] * turn_e(v) - low_w[level] * turn_w(v)
         total = total + (up_n[level] * v_n - low_s[level] * v_s)
-        return with_levels(total, level, below, above)
-
-    def adjoint_sum(level, v, below, above):
-        total = up_w[level] * to_w(v) - low_e[level] * to_e(v)
-        total = total + (up_s[level] * to_s(v) - low_n[level] * to_n(v))
-        return with_levels(total, level, below, above)
-
-    def sweep(field, body):
-        below, here = None, field[0]
-        for level in range(levels):
-            above = field[level + 1] if level + 1 < levels else None
-            body(level, here, below, above)
-            below, here = here, above
+        return with_levels(level_ref, total, level, below, above)
 
     for level in range(levels):
         ed = gather(ED, level)
@@ -246,9 +266,9 @@
         far_nw = wide(far_south(2 * levels + level)) * 0.5
         first = rows == 0
         e_low, e_up, n_low, n_up = ew + ed, ew - ed, nw + nd, nw - nd
-        w_low, w_up = to_w(e_low), to_w(e_up)
-        s_low = jnp.where(first, far_nw + far_nd, to_s(n_low))
-        s_up = jnp.where(first, far_nw - far_nd, to_s(n_up))
+        w_low, w_up = turn_w(e_low), turn_w(e_up)
+        s_low = jnp.where(first, far_nw + far_nd, turn_s(n_low))
+        s_up = jnp.where(first, far_nw - far_nd, turn_s(n_up))
         up_e[level] = e_up
         low_e[level] = e_low
         up_w[level] = w_up
@@ -257,23 +277,11 @@
         low_n[level] = n_low
         up_s[level] = s_up
         low_s[level] = s_low
-        center = (e_low - w_up) + (n_low - s_up) + pair(level)
-        a_c[level] = center
-        base = ed + to_w(ed) + nd + jnp.where(first, far_nd, to_s(nd)) + (1.0 + pair(level))
-        diag[level] = base
+        pair = level_pair(level_ref, level, levels)
+        a_c[level] = (e_low - w_up) + (n_low - s_up) + pair
+        diag[level] = ed + turn_w(ed) + nd + jnp.where(first, far_nd, turn_s(nd)) + (1.0 + pair)
         check[level] = gather(C, level)
         force[level] = gather(S, level) * cos_ref[...]
-        tangent = jnp.tanh(gather(TR, level))
-        local = damp_ref[level] * (1.0 - tangent * tangent)
-        weight_a = RELAXATION / (base + local)
-        af = gather(AF, level)
-        diagonal = 1.0 + center + local
-        aq_a[level] = diagonal
-        wt_a[level] = weight_a
-        ctr_a[level] = 1.0 - weight_a * diagonal
-        start = weight_a * af
-        g_a[level] = start
-        d_a[level] = start
 
     def newton(level, resid, tangent):
         local = damp_ref[level] * (1.0 - tangent * tangent)
@@ -286,8 +294,8 @@
 
     def first_resid(level, v, below, above):
         tangent = jnp.tanh(v)
-        v_s = jnp.where(rows == 0, wide(far_south(level)), to_s(v))
-        v_n = jnp.where(rows == 23, wide(far_north(level)), to_n(v))
+        v_s = jnp.where(rows == 0, wide(far_south(level)), turn_s(v))
+        v_n = jnp.where(rows == 23, wide(far_north(level)), turn_n(v))
         total = forward_sum(level, v, below, above, v_n, v_s)
         resid = total + a_c[level] * v + damp_ref[level] * tangent - force[level]
         newton(level, resid, tangent)
@@ -295,25 +303,6 @@
     def forward_lin(level, v, below, above):
         total = forward_sum(level, v, below, above)
         d[level] = g[level] + ctr[level] * v - wt[level] * total
-
-    def adjoint_lin(level, v, below, above):
-        total = adjoint_sum(level, v, below, above)
-        d_a[level] = g_a[level] + ctr_a[level] * v - wt_a[level] * total
-
-    def relax(field, body):
-        def step(_, carry):
-            sweep(field, body)
-            return carry
-
-        lax.fori_loop(0, 3, step, 0)
-
-    sweep(check, first_resid)
-    relax(d, forward_lin)
-
-    relax(d_a, adjoint_lin)
-    for level in range(levels):
-        x[level] = check[level] + d[level]
-        mu[level] = d_a[level]
 
     def second_resid(level, v, below, above):
         tangent = jnp.tanh(v)
@@ -322,32 +311,100 @@
         resid = moved + total + a_c[level] * v + damp_ref[level] * tangent - force[level]
         newton(level, resid, tangent)
 
-    def adjoint_resid(level, v, below, above):
-        total = adjoint_sum(level, v, below, above)
-        af = g_a[level]
-        start = af - wt_a[level] * (total + aq_a[level] * v)
-        g_a[level] = start
-        d_a[level] = start
-
-    sweep(x, second_resid)
-    relax(d, forward_lin)
-    sweep(mu, adjoint_resid)
-    relax(d_a, adjoint_lin)
-    for level in range(levels):
-        final = x[level] + d[level]
-        x[level] = final
-        state = final[8:16, :128]
-        out_state[level] = state
-        multiplier = mu[level, 8:16, :128] + d_a[level, 8:16, :128]
-        out_adjoint[level] = multiplier + weight[level] * (state - observations[level])
-
     def final_resid(level, v, below, above):
         total = forward_sum(level, v, below, above)
         moved = v - check[level]
         resid = moved + total + a_c[level] * v + damp_ref[level] * jnp.tanh(v) - force[level]
         out_resid[level] = resid[8:16, :128]
 
+    sweep(check, first_resid)
+    relax(d, forward_lin)
+    for level in range(levels):
+        x[level] = check[level] + d[level]
+    sweep(x, second_resid)
+    relax(d, forward_lin)
+    for level in range(levels):
+        final = x[level] + d[level]
+        x[level] = final
+        out_state[level] = final[8:16, :128]
+        keep_state[level] = final[8:16, :128]
     sweep(x, final_resid)
+
+
+def adjoint_kernel(
+    y_ref,
+    level_ref,
+    damp_ref,
+    own,
+    adjoint_odd,
+    from_even,
+    corner_own,
+    corner_odd,
+    corner_even,
+    state,
+    a_c,
+    diag,
+    low_e,
+    up_w,
+    low_n,
+    up_s,
+    observations,
+    weight,
+    out_adjoint,
+    aq,
+    wt,
+    ctr,
+    g,
+    d,
+    mu,
+):
+    levels = mu.shape[0]
+    gather, _, _ = gatherer(
+        y_ref[0] % 2 == 1,
+        own,
+        lambda k, at: adjoint_odd[k - FORWARD, at],
+        from_even,
+        corner_own,
+        corner_odd,
+        corner_even,
+        None,
+    )
+
+    def adjoint_sum(level, v, below, above):
+        total = up_w[level] * turn_w(v) - low_e[level] * turn_e(v)
+        total = total + (up_s[level] * turn_s(v) - low_n[level] * turn_n(v))
+        return with_levels(level_ref, total, level, below, above)
+
+    for level in range(levels):
+        tangent = jnp.tanh(gather(TR, level))
+        local = damp_ref[level] * (1.0 - tangent * tangent)
+        w = RELAXATION / (diag[level] + local)
+        diagonal = 1.0 + a_c[level] + local
+        aq[level] = diagonal
+        wt[level] = w
+        ctr[level] = 1.0 - w * diagonal
+        start = w * gather(AF, level)
+        g[level] = start
+        d[level] = start
+
+    def adjoint_lin(level, v, below, above):
+        total = adjoint_sum(level, v, below, above)
+        d[level] = g[level] + ctr[level] * v - wt[level] * total
+
+    def adjoint_resid(level, v, below, above):
+        total = adjoint_sum(level, v, below, above)
+        start = g[level] - wt[level] * (total + aq[level] * v)
+        g[level] = start
+        d[level] = start
+
+    relax(d, adjoint_lin)
+    for level in range(levels):
+        mu[level] = d[level]
+    sweep(mu, adjoint_resid)
+    relax(d, adjoint_lin)
+    for level in range(levels):
+        multiplier = mu[level, 8:16, :128] + d[level, 8:16, :128]
+        out_adjoint[level] = multiplier + weight[level] * (state[level] - observations[level])
 
 
 def vmem(count):
@@ -397,12 +454,14 @@
     f32 = jnp.float32
     smem = pl.BlockSpec(memory_space=pltpu.SMEM)
     strip = (levels // 2 + 1, lat_rows, lon_cols)
-    block, strip_odd, strip_even = pl.pallas_call(
+    block, block_f, block_a, strip_odd, strip_even = pl.pallas_call(
         functools.partial(pack_kernel, size_y),
         in_specs=[smem, smem] + vmem(8),
-        out_specs=vmem(3),
+        out_specs=vmem(5),
         out_shape=[
             pltpu.VMEM((FIELDS,) + tile, f32),
+            pltpu.VMEM((FORWARD,) + tile, f32),
+            pltpu.VMEM((FIELDS - FORWARD,) + tile, f32),
             pltpu.VMEM(strip, f32),
             pltpu.VMEM(strip, f32),
         ],
@@ -418,7 +477,7 @@
         trajectory,
         adjoint_forcing,
     )
-    from_odd = swap(block, "gy", 1, 1, False)
+    from_odd = swap(block_f, "gy", 1, 1, False)
     from_even = swap(block, "gy", 0, 1, False)
     lon_odd = swap(strip_odd, "gx", 1, 1, True)
     lon_even = swap(strip_even, "gx", 0, 1, True)
@@ -443,31 +502,54 @@
         compiler_params=small,
     )(place_y, corners, from_odd)
     corner_even = swap(corners_b, "gy", 0, 1, False)
-    scratch = [pltpu.VMEM((levels, 24, 256), f32) for _ in range(23)]
-    return tuple(
-        pl.pallas_call(
-            solve_kernel,
-            in_specs=[smem, smem, smem] + vmem(10),
-            out_specs=vmem(3),
-            out_shape=[jax.ShapeDtypeStruct(tile, f32)] * 3,
-            scratch_shapes=scratch,
-            compiler_params=pltpu.CompilerParams(vmem_limit_bytes=20 * 1024 * 1024),
-        )(
-            place_y,
-            level_diffusion,
-            damping,
-            wave,
-            block,
-            from_odd,
-            from_even,
-            corners,
-            corner_odd,
-            corner_even,
-            rims,
-            observations,
-            observation_weight,
-        )
-    )
+    adjoint_odd = swap(block_a, "gy", 1, 1, False)
+    wide = (levels, 3 * lat_rows, 2 * lon_cols)
+    large = pltpu.CompilerParams(vmem_limit_bytes=16 * 1024 * 1024)
+    state, resid, keep_state, *coefs = pl.pallas_call(
+        forward_kernel,
+        in_specs=[smem] * 3 + vmem(8),
+        out_specs=vmem(9),
+        out_shape=[jax.ShapeDtypeStruct(tile, f32)] * 2
+        + [pltpu.VMEM(tile, f32)]
+        + [pltpu.VMEM(wide, f32)] * 6,
+        scratch_shapes=[pltpu.VMEM(wide, f32) for _ in range(11)],
+        compiler_params=large,
+    )(
+        place_y,
+        level_diffusion,
+        damping,
+        wave,
+        block,
+        from_odd,
+        from_even,
+        corners,
+        corner_odd,
+        corner_even,
+        rims,
+    )
+    result = pl.pallas_call(
+        adjoint_kernel,
+        in_specs=[smem] * 3 + vmem(15),
+        out_specs=vmem(1)[0],
+        out_shape=jax.ShapeDtypeStruct(tile, f32),
+        scratch_shapes=[pltpu.VMEM(wide, f32) for _ in range(6)],
+        compiler_params=large,
+    )(
+        place_y,
+        level_diffusion,
+        damping,
+        block,
+        adjoint_odd,
+        from_even,
+        corners,
+        corner_odd,
+        corner_even,
+        keep_state,
+        *coefs,
+        observations,
+        observation_weight,
+    )
+    return state, resid, result
 
 
 def solution(mesh):

time: 59.8 us -> 59.1 us (0.988)
  waiting for transfers between devices: 13.6 us -> 9.27 us
  starting transfers between devices: 34.5 us -> 36.8 us
  Pallas kernels: 9.9 us -> 11.2 us
    ppermute x6 -> x7, waiting for transfers between devices: 13.6 us -> 9.27 us  [swap(): return lax.ppermute(array, axis, pairs)]
    ppermute x6 -> x7, starting transfers between devices: 34.5 us -> 36.8 us  [swap(): return lax.ppermute(array, axis, pairs)]
    pallas_call x1 -> x2, Pallas kernels: 8.4 us -> 9.69 us  [the longest x1 5.93 us: compute(): pl.pallas_call(forward_kernel, in_specs=[smem] * 3 + vmem(8), out_specs=v...]
  transfers between devices with their start and end apart: 6 -> 7, of which waited for: 2 -> 3; matrix products, arithmetic and copies ran while one was open for 0% -> 0% of each run, Pallas kernels for 0% -> 10%
where the time goes in v3:
time: 59.1 us; the launch traced here: 58.7 us
  starting transfers between devices  36.8 us (62%)
  Pallas kernels  11.2 us (19%)
  waiting for transfers between devices  9.27 us (16%)
  between operations  1.41 us (2%)
    ppermute x7, starting transfers between devices, swap(): return lax.ppermute(array, axis, pairs)  36.8 us
    ppermute x7, waiting for transfers between devices, swap(): return lax.ppermute(array, axis, pairs)  9.27 us
    pallas_call x1, Pallas kernels, compute(): pl.pallas_call(forward_kernel, in_specs=[smem] * 3 + vmem(8), out_specs=v...  5.93 us
    pallas_call x1, Pallas kernels, compute(): pl.pallas_call(adjoint_kernel, in_specs=[smem] * 3 + vmem(15), out_specs=...  3.76 us
    pallas_call x1, Pallas kernels, compute(): pl.pallas_call(functools.partial(pack_kernel, size_y), in_specs=[smem, sm...  1.47 us
  transfers between devices with their start and end apart: 7, of which 3 were waited for; matrix products, arithmetic and copies ran while one was open for 0% of the time, Pallas kernels for 10%

profile of v3, /device:TPU:6, one launch (start us, length us, event | category | flops | bytes accessed | tf_op | source)
XLA Modules:
  0.0 58.7 jit_solution(9206790728013240876)
XLA Ops:
  0.6 1.5 %shard_map.148 = (f32[8,16,8,128]{3,2,1,0:T(8,128)S(1)}, f32[6,16,8,128]{3,2,1,0:T(8,128)S(1)}, f32[2,16,8,128]{3,2,1,0:T(8,128)S(1)}, f32[9,8,128]{2,1,0:T(8,128)S(1)}, f32[9,8,128]{2,1,0:T(8,128)S(1)}) custom-call(s32[1]{0:T(128)} %bitcast.2.x_ref, s32[1]{0:T(128)} %bitcast.y_ref, f32[16,8,128]{2,1,0:T(8,128)} %refs_0_.1, f32[16,8,128]{2,1,0:T(8,128)} %refs_1_.1, ...), custom_call_target="tpu_custom_call" | custom-call | tf_op jit(solution)/shard_map/pallas_call | solution.py:457
  2.1 1.9 %collective-permute-start.1 = (f32[8,16,8,128]{3,2,1,0:T(8,128)S(1)}, f32[8,16,8,128]{3,2,1,0:T(8,128)S(1)}, u32[]{:S(2)}, u32[]{:S(2)}) collective-permute-start(f32[8,16,8,128]{3,2,1,0:T(8,128)S(1)} %get-tuple-element.19.own), channel_id=1, source_target_pairs={{0,1},{1,0},{2,3},{3,2},{4,5},{5,4},{6,7},{7,6},{8,9},{9,8},{10,11... | collective-permute-start | bytes 1572872 | tf_op jit(solution)/shard_map/ppermute | solution.py:421
  4.0 8.3 %collective-permute-start = (f32[6,16,8,128]{3,2,1,0:T(8,128)S(1)}, f32[6,16,8,128]{3,2,1,0:T(8,128)S(1)}, u32[]{:S(2)}, u32[]{:S(2)}) collective-permute-start(f32[6,16,8,128]{3,2,1,0:T(8,128)S(1)} %get-tuple-element.20), channel_id=1, source_target_pairs={{1,2},{2,1},{3,4},{4,3},{5,6},{6,5},{7,8},{8,7},{9,10},{10,9},{11,... | collective-permute-start | bytes 1179656 | tf_op jit(solution)/shard_map/ppermute | solution.py:421
  12.3 18.4 %collective-permute-start.2 = (f32[9,8,128]{2,1,0:T(8,128)S(1)}, f32[9,8,128]{2,1,0:T(8,128)S(1)}, u32[]{:S(2)}, u32[]{:S(2)}) collective-permute-start(f32[9,8,128]{2,1,0:T(8,128)S(1)} %get-tuple-element.21), channel_id=1, source_target_pairs={{32,64},{64,32},{96,128},{128,96},{160,192},{192,160},{224,256},{2... | collective-permute-start | bytes 110600 | tf_op jit(solution)/shard_map/ppermute | solution.py:421
  30.7 1.9 %collective-permute-start.3 = (f32[9,8,128]{2,1,0:T(8,128)S(1)}, f32[9,8,128]{2,1,0:T(8,128)S(1)}, u32[]{:S(2)}, u32[]{:S(2)}) collective-permute-start(f32[9,8,128]{2,1,0:T(8,128)S(1)} %get-tuple-element.22), channel_id=1, source_target_pairs={{0,32},{32,0},{64,96},{96,64},{128,160},{160,128},{192,224},{224,1... | collective-permute-start | bytes 110600 | tf_op jit(solution)/shard_map/ppermute | solution.py:421
  32.7 2.4 %collective-permute-start.6 = (f32[2,16,8,128]{3,2,1,0:T(8,128)S(1)}, f32[2,16,8,128]{3,2,1,0:T(8,128)S(1)}, u32[]{:S(2)}, u32[]{:S(2)}) collective-permute-start(f32[2,16,8,128]{3,2,1,0:T(8,128)S(1)} %get-tuple-element.27), channel_id=1, source_target_pairs={{1,2},{2,1},{3,4},{4,3},{5,6},{6,5},{7,8},{8,7},{9,10},{10,9},{11,... | collective-permute-start | bytes 393224 | tf_op jit(solution)/shard_map/ppermute | solution.py:421
  35.7 4.7 %collective-permute-done.2.from_odd = f32[9,8,128]{2,1,0:T(8,128)S(1)} collective-permute-done((f32[9,8,128]{2,1,0:T(8,128)S(1)}, f32[9,8,128]{2,1,0:T(8,128)S(1)}, u32[]{:S(2)}, u32[]{:S(2)}) %collective-permute-start.2) | collective-permute-done | bytes 36896 | tf_op jit(solution)/shard_map/ppermute | solution.py:421
  40.4 0.0 collective-permute-done.3.from_even
  40.4 0.0 collective-permute-done.1.block_even.from_even
  40.5 1.9 %collective-permute-start.4 = (f32[22,8,128]{2,1,0:T(8,128)S(1)}, f32[22,8,128]{2,1,0:T(8,128)S(1)}, u32[]{:S(2)}, u32[]{:S(2)}) collective-permute-start(f32[22,8,128]{2,1,0:T(8,128)S(1)} %get-tuple-element.23.corner_own), channel_id=1, source_target_pairs={{1,2},{2,1},{3,4},{4,3},{5,6},{6,5},{7,8},{8,7},{9,10},{10,9},{11,... | collective-permute-start | bytes 270344 | tf_op jit(solution)/shard_map/ppermute | solution.py:421
  42.4 0.0 collective-permute-done.block_odd.from_odd
  42.5 1.9 %collective-permute-start.5 = (f32[22,8,128]{2,1,0:T(8,128)S(1)}, f32[22,8,128]{2,1,0:T(8,128)S(1)}, u32[]{:S(2)}, u32[]{:S(2)}) collective-permute-start(f32[22,8,128]{2,1,0:T(8,128)S(1)} %shard_map.150), channel_id=1, source_target_pairs={{0,1},{1,0},{2,3},{3,2},{4,5},{5,4},{6,7},{7,6},{8,9},{9,8},{10,11... | collective-permute-start | bytes 270344 | tf_op jit(solution)/shard_map/ppermute | solution.py:421
  44.4 0.1 fusion.4.cos_ref
  44.4 0.0 copy-start.2
  44.5 0.0 copy-start.3
  44.5 1.2 %collective-permute-done.5.corner_even = f32[22,8,128]{2,1,0:T(8,128)S(1)} collective-permute-done((f32[22,8,128]{2,1,0:T(8,128)S(1)}, f32[22,8,128]{2,1,0:T(8,128)S(1)}, u32[]{:S(2)}, u32[]{:S(2)}) %collective-permute-start.5) | collective-permute-done | bytes 90144 | tf_op jit(solution)/shard_map/ppermute | solution.py:421
  45.6 3.4 %collective-permute-done.4.corner_odd = f32[22,8,128]{2,1,0:T(8,128)S(1)} collective-permute-done((f32[22,8,128]{2,1,0:T(8,128)S(1)}, f32[22,8,128]{2,1,0:T(8,128)S(1)}, u32[]{:S(2)}, u32[]{:S(2)}) %collective-permute-start.4) | collective-permute-done | bytes 90144 | tf_op jit(solution)/shard_map/ppermute | solution.py:421
  49.0 0.0 copy-done.2
  49.0 0.0 copy-done.3
  49.0 0.0 copy-start
  49.0 0.0 copy-start.1
  49.0 5.9 %shard_map.151 = (f32[16,8,128]{2,1,0:T(8,128)}, f32[16,8,128]{2,1,0:T(8,128)}, f32[16,8,128]{2,1,0:T(8,128)S(1)}, f32[16,24,256]{2,1,0:T(8,128)S(1)}, f32[16,24...) custom-call(s32[1]{0:T(128)} %bitcast.y_ref, ...), custom_call_target="tpu_custom_call" | custom-call | tf_op jit(solution)/shard_map/pallas_call | solution.py:508
  55.0 0.0 collective-permute-done.6.adjoint_odd
  55.0 0.0 copy-done
  55.0 0.0 copy-done.1
  55.0 3.8 %shard_map.152 = f32[16,8,128]{2,1,0:T(8,128)} custom-call(s32[1]{0:T(128)} %bitcast.y_ref, f32[16]{0:T(128)S(1)} %copy-done.2, f32[16]{0:T(128)S(1)} %copy-done.3, f32[8,16,8,128]{3,2,1,0:T(8,128)S(1)} %get-tuple-element.19.own, f32[2,16,8,128]{3,2,1,0:T(8,128)S(1)} %collective-permute-done.6.adjoint_odd, ...), custom_call_target="tpu_custom_call" | custom-call | tf_op jit(solution)/shard_map/pallas_call | solution.py:530
  (2 shorter events, 0.1 us)
Async XLA Ops:
  2.1 38.3 %collective-permute-start.1 = (f32[8,16,8,128]{3,2,1,0:T(8,128)S(1)}, f32[8,16,8,128]{3,2,1,0:T(8,128)S(1)}, u32[]{:S(2)}, u32[]{:S(2)}) collective-permute-start(f32[8,16,8,128]{3,2,1,0:T(8,128)S(1)} %get-tuple-element.19.own), channel_id=1, source_target_pairs={{0,1},{1,0},{2,3},{3,2},{4,5},{5,4},{6,7},{7,6},{8,9},{9,8},{10,11... | collective-permute-start | bytes 1572872 | tf_op jit(solution)/shard_map/ppermute | solution.py:421
  4.0 38.4 %collective-permute-start = (f32[6,16,8,128]{3,2,1,0:T(8,128)S(1)}, f32[6,16,8,128]{3,2,1,0:T(8,128)S(1)}, u32[]{:S(2)}, u32[]{:S(2)}) collective-permute-start(f32[6,16,8,128]{3,2,1,0:T(8,128)S(1)} %get-tuple-element.20), channel_id=1, source_target_pairs={{1,2},{2,1},{3,4},{4,3},{5,6},{6,5},{7,8},{8,7},{9,10},{10,9},{11,... | collective-permute-start | bytes 1179656 | tf_op jit(solution)/shard_map/ppermute | solution.py:421
  12.3 28.1 %collective-permute-start.2 = (f32[9,8,128]{2,1,0:T(8,128)S(1)}, f32[9,8,128]{2,1,0:T(8,128)S(1)}, u32[]{:S(2)}, u32[]{:S(2)}) collective-permute-start(f32[9,8,128]{2,1,0:T(8,128)S(1)} %get-tuple-element.21), channel_id=1, source_target_pairs={{32,64},{64,32},{96,128},{128,96},{160,192},{192,160},{224,256},{2... | collective-permute-start | bytes 110600 | tf_op jit(solution)/shard_map/ppermute | solution.py:421
  30.7 9.7 %collective-permute-start.3 = (f32[9,8,128]{2,1,0:T(8,128)S(1)}, f32[9,8,128]{2,1,0:T(8,128)S(1)}, u32[]{:S(2)}, u32[]{:S(2)}) collective-permute-start(f32[9,8,128]{2,1,0:T(8,128)S(1)} %get-tuple-element.22), channel_id=1, source_target_pairs={{0,32},{32,0},{64,96},{96,64},{128,160},{160,128},{192,224},{224,1... | collective-permute-start | bytes 110600 | tf_op jit(solution)/shard_map/ppermute | solution.py:421
  32.7 22.3 %collective-permute-start.6 = (f32[2,16,8,128]{3,2,1,0:T(8,128)S(1)}, f32[2,16,8,128]{3,2,1,0:T(8,128)S(1)}, u32[]{:S(2)}, u32[]{:S(2)}) collective-permute-start(f32[2,16,8,128]{3,2,1,0:T(8,128)S(1)} %get-tuple-element.27), channel_id=1, source_target_pairs={{1,2},{2,1},{3,4},{4,3},{5,6},{6,5},{7,8},{8,7},{9,10},{10,9},{11,... | collective-permute-start | bytes 393224 | tf_op jit(solution)/shard_map/ppermute | solution.py:421
  40.5 8.5 %collective-permute-start.4 = (f32[22,8,128]{2,1,0:T(8,128)S(1)}, f32[22,8,128]{2,1,0:T(8,128)S(1)}, u32[]{:S(2)}, u32[]{:S(2)}) collective-permute-start(f32[22,8,128]{2,1,0:T(8,128)S(1)} %get-tuple-element.23.corner_own), channel_id=1, source_target_pairs={{1,2},{2,1},{3,4},{4,3},{5,6},{6,5},{7,8},{8,7},{9,10},{10,9},{11,... | collective-permute-start | bytes 270344 | tf_op jit(solution)/shard_map/ppermute | solution.py:421
  42.5 3.2 %collective-permute-start.5 = (f32[22,8,128]{2,1,0:T(8,128)S(1)}, f32[22,8,128]{2,1,0:T(8,128)S(1)}, u32[]{:S(2)}, u32[]{:S(2)}) collective-permute-start(f32[22,8,128]{2,1,0:T(8,128)S(1)} %shard_map.150), channel_id=1, source_target_pairs={{0,1},{1,0},{2,3},{3,2},{4,5},{5,4},{6,7},{7,6},{8,9},{9,8},{10,11... | collective-permute-start | bytes 270344 | tf_op jit(solution)/shard_map/ppermute | solution.py:421
  44.4 4.6 %copy-start.2 = (f32[16]{0:T(128)S(1)}, f32[16]{0:T(128)}, u32[]{:S(2)}) copy-start(f32[16]{0:T(128)} %level_ref.3) | copy-start | bytes 196
  44.5 4.6 %copy-start.3 = (f32[16]{0:T(128)S(1)}, f32[16]{0:T(128)}, u32[]{:S(2)}) copy-start(f32[16]{0:T(128)} %damp_ref.3) | copy-start | bytes 196
  49.0 5.9 %copy-start = (f32[16,8,128]{2,1,0:T(8,128)S(1)}, f32[16,8,128]{2,1,0:T(8,128)}, u32[]{:S(2)}) copy-start(f32[16,8,128]{2,1,0:T(8,128)} %observations.1) | copy-start | bytes 196612
  49.0 5.9 %copy-start.1 = (f32[16,8,128]{2,1,0:T(8,128)S(1)}, f32[16,8,128]{2,1,0:T(8,128)}, u32[]{:S(2)}) copy-start(f32[16,8,128]{2,1,0:T(8,128)} %weight.1) | copy-start | bytes 196612

commit v4 on v2

--- a/solution.py
+++ b/solution.py
@@ -112,32 +112,30 @@
     out_resid,
     out_adjoint,
     check,
+    d,
+    x,
+    d_a,
+    mu,
+    up_n,
+    low_n,
+    north,
     force,
     a_c,
     diag,
     up_e,
     low_w,
-    up_n,
-    low_s,
     low_e,
     up_w,
-    low_n,
-    up_s,
     wt,
     ctr,
     g,
-    d,
-    x,
     aq_a,
     wt_a,
     ctr_a,
     g_a,
-    d_a,
-    mu,
 ):
     levels = check.shape[0]
     lanes = lane_ids()
-    rows = lax.broadcasted_iota(jnp.int32, (24, 256), 0)
 
     half = levels // 2
     odd_y = y_ref[0] % 2 == 1
@@ -179,15 +177,17 @@
         right = turned(east, -base)
         return jnp.where(lanes < SLOT, right, jnp.where(lanes >= 128 - SLOT, left, 0.0))
 
-    def gather(k, level):
+    def strips(level):
         place = level % half
+        pairs = []
+        for side in (side_south, side_own, side_north):
+            pairs.append((side(place), side(half + place)))
+        return pairs
+
+    def gather(k, level, pairs):
         tiles = []
-        for tile, strip in (
-            (tile_south, side_south),
-            (tile_own, side_own),
-            (tile_north, side_north),
-        ):
-            side = halo(k, level, strip(place), strip(half + place))
+        for tile, (west, east) in zip((tile_south, tile_own, tile_north), pairs):
+            side = halo(k, level, west, east)
             if tile is tile_own:
                 if k == C:
                     side = jnp.where(lanes == SLOT, turned(rims[1], SLOT - level), side)
@@ -198,21 +198,28 @@
             tiles.append(jnp.concatenate([tile(k, level), side], axis=1))
         return jnp.concatenate(tiles, axis=0)
 
-    def wide(line):
-        line = jnp.concatenate([line, jnp.zeros_like(line)], axis=1)
-        return jnp.broadcast_to(line, (24, 256))
+    def rows_of(ref, level, first):
+        parts = [ref[level, side, first : first + 24] for side in range(2)]
+        return jnp.concatenate(parts, axis=1)
+
+    def middle(ref, level):
+        return rows_of(ref, level, 8)
+
+    def to_n(ref, level):
+        return rows_of(ref, level, 9)
+
+    def to_s(ref, level):
+        return rows_of(ref, level, 7)
+
+    def keep(ref, level, value):
+        ref[level, 0, 8:32] = value[:, :128]
+        ref[level, 1, 8:32] = value[:, 128:]
 
     def to_e(v):
         return pltpu.roll(v, 255, 1)
 
     def to_w(v):
         return pltpu.roll(v, 1, 1)
-
-    def to_n(v):
-        return pltpu.roll(v, 23, 0)
-
-    def to_s(v):
-        return pltpu.roll(v, 1, 0)
 
     def up(level):
         return level_ref[level] if level < levels - 1 else None
@@ -231,62 +238,71 @@
             total = total - down(level) * below
         return total
 
-    def forward_sum(level, v, below, above, v_n=None, v_s=None):
-        v_n = to_n(v) if v_n is None else v_n
-        v_s = to_s(v) if v_s is None else v_s
+    def forward_sum(field, level, v, below, above):
         total = up_e[level] * to_e(v) - low_w[level] * to_w(v)
-        total = total + (up_n[level] * v_n - low_s[level] * v_s)
+        rows_n = middle(up_n, level) * to_n(field, level)
+        total = total + (rows_n - to_s(low_n, level) * to_s(field, level))
         return with_levels(total, level, below, above)
 
-    def adjoint_sum(level, v, below, above):
+    def adjoint_sum(field, level, v, below, above):
         total = up_w[level] * to_w(v) - low_e[level] * to_e(v)
-        total = total + (up_s[level] * to_s(v) - low_n[level] * to_n(v))
+        rows_s = to_s(up_n, level) * to_s(field, level)
+        total = total + (rows_s - middle(low_n, level) * to_n(field, level))
         return with_levels(total, level, below, above)
 
     def sweep(field, body):
-        below, here = None, field[0]
+        below, here = None, middle(field, 0)
         for level in range(levels):
-            above = field[level + 1] if level + 1 < levels else None
-            body(level, here, below, above)
+            above = middle(field, level + 1) if level + 1 < levels else None
+            body(field, level, here, below, above)
             below, here = here, above
 
+    blank = jnp.zeros((8, 128), jnp.float32)
+    for ref in (check, d, x, d_a, mu, up_n, low_n, north):
+        for level in range(levels):
+            for side in range(2):
+                ref[level, side, 0:8] = blank
+                ref[level, side, 32:40] = blank
+
     for level in range(levels):
-        ed = gather(ED, level)
-        ew = gather(EW, level) * 0.5
-        nd = gather(ND, level)
-        nw = gather(NW, level) * 0.5
-        far_nd = wide(far_south(levels + level))
-        far_nw = wide(far_south(2 * levels + level)) * 0.5
-        first = rows == 0
+        pairs = strips(level)
+        ed = gather(ED, level, pairs)
+        ew = gather(EW, level, pairs) * 0.5
+        nd = gather(ND, level, pairs)
+        nw = gather(NW, level, pairs) * 0.5
+        far_nd = far_south(levels + level)
+        far_nw = far_south(2 * levels + level) * 0.5
         e_low, e_up, n_low, n_up = ew + ed, ew - ed, nw + nd, nw - nd
+        keep(up_n, level, n_up)
+        keep(low_n, level, n_low)
+        keep(north, level, nd)
+        up_n[level, 0, 7:8] = far_nw - far_nd
+        low_n[level, 0, 7:8] = far_nw + far_nd
+        north[level, 0, 7:8] = far_nd
         w_low, w_up = to_w(e_low), to_w(e_up)
-        s_low = jnp.where(first, far_nw + far_nd, to_s(n_low))
-        s_up = jnp.where(first, far_nw - far_nd, to_s(n_up))
         up_e[level] = e_up
         low_e[level] = e_low
         up_w[level] = w_up
         low_w[level] = w_low
-        up_n[level] = n_up
-        low_n[level] = n_low
-        up_s[level] = s_up
-        low_s[level] = s_low
-        center = (e_low - w_up) + (n_low - s_up) + pair(level)
+        center = (e_low - w_up) + (n_low - to_s(up_n, level)) + pair(level)
         a_c[level] = center
-        base = ed + to_w(ed) + nd + jnp.where(first, far_nd, to_s(nd)) + (1.0 + pair(level))
+        base = ed + to_w(ed) + nd + to_s(north, level) + (1.0 + pair(level))
         diag[level] = base
-        check[level] = gather(C, level)
-        force[level] = gather(S, level) * cos_ref[...]
-        tangent = jnp.tanh(gather(TR, level))
+        keep(check, level, gather(C, level, pairs))
+        check[level, 0, 7:8] = far_south(level)
+        check[level, 0, 32:33] = far_north(level)
+        force[level] = gather(S, level, pairs) * cos_ref[...]
+        tangent = jnp.tanh(gather(TR, level, pairs))
         local = damp_ref[level] * (1.0 - tangent * tangent)
         weight_a = RELAXATION / (base + local)
-        af = gather(AF, level)
+        af = gather(AF, level, pairs)
         diagonal = 1.0 + center + local
         aq_a[level] = diagonal
         wt_a[level] = weight_a
         ctr_a[level] = 1.0 - weight_a * diagonal
         start = weight_a * af
         g_a[level] = start
-        d_a[level] = start
+        keep(d_a, level, start)
 
     def newton(level, resid, tangent):
         local = damp_ref[level] * (1.0 - tangent * tangent)
@@ -295,23 +311,21 @@
         ctr[level] = 1.0 - w * (1.0 + a_c[level] + local)
         start = -(w * resid)
         g[level] = start
-        d[level] = start
-
-    def first_resid(level, v, below, above):
+        keep(d, level, start)
+
+    def first_resid(field, level, v, below, above):
         tangent = jnp.tanh(v)
-        v_s = jnp.where(rows == 0, wide(far_south(level)), to_s(v))
-        v_n = jnp.where(rows == 23, wide(far_north(level)), to_n(v))
-        total = forward_sum(level, v, below, above, v_n, v_s)
+        total = forward_sum(field, level, v, below, above)
         resid = total + a_c[level] * v + damp_ref[level] * tangent - force[level]
         newton(level, resid, tangent)
 
-    def forward_lin(level, v, below, above):
-        total = forward_sum(level, v, below, above)
-        d[level] = g[level] + ctr[level] * v - wt[level] * total
-
-    def adjoint_lin(level, v, below, above):
-        total = adjoint_sum(level, v, below, above)
-        d_a[level] = g_a[level] + ctr_a[level] * v - wt_a[level] * total
+    def forward_lin(field, level, v, below, above):
+        total = forward_sum(field, level, v, below, above)
+        keep(field, level, g[level] + ctr[level] * v - wt[level] * total)
+
+    def adjoint_lin(field, level, v, below, above):
+        total = adjoint_sum(field, level, v, below, above)
+        keep(field, level, g_a[level] + ctr_a[level] * v - wt_a[level] * total)
 
     def relax(field, body):
         def step(_, carry):
@@ -322,41 +336,39 @@
 
     sweep(check, first_resid)
     relax(d, forward_lin)
-
     relax(d_a, adjoint_lin)
     for level in range(levels):
-        x[level] = check[level] + d[level]
-        mu[level] = d_a[level]
-
-    def second_resid(level, v, below, above):
+        keep(x, level, middle(check, level) + middle(d, level))
+        keep(mu, level, middle(d_a, level))
+
+    def second_resid(field, level, v, below, above):
         tangent = jnp.tanh(v)
-        total = forward_sum(level, v, below, above)
-        moved = v - check[level]
+        total = forward_sum(field, level, v, below, above)
+        moved = v - middle(check, level)
         resid = moved + total + a_c[level] * v + damp_ref[level] * tangent - force[level]
         newton(level, resid, tangent)
 
-    def adjoint_resid(level, v, below, above):
-        total = adjoint_sum(level, v, below, above)
-        af = g_a[level]
-        start = af - wt_a[level] * (total + aq_a[level] * v)
+    def adjoint_resid(field, level, v, below, above):
+        total = adjoint_sum(field, level, v, below, above)
+        start = g_a[level] - wt_a[level] * (total + aq_a[level] * v)
         g_a[level] = start
-        d_a[level] = start
+        keep(d_a, level, start)
 
     sweep(x, second_resid)
     relax(d, forward_lin)
     sweep(mu, adjoint_resid)
     relax(d_a, adjoint_lin)
     for level in range(levels):
-        final = x[level] + d[level]
-        x[level] = final
+        final = middle(x, level) + middle(d, level)
+        keep(x, level, final)
         state = final[8:16, :128]
         out_state[level] = state
-        multiplier = mu[level, 8:16, :128] + d_a[level, 8:16, :128]
+        multiplier = mu[level, 0, 16:24] + d_a[level, 0, 16:24]
         out_adjoint[level] = multiplier + weight[level] * (state - observations[level])
 
-    def final_resid(level, v, below, above):
-        total = forward_sum(level, v, below, above)
-        moved = v - check[level]
+    def final_resid(field, level, v, below, above):
+        total = forward_sum(field, level, v, below, above)
+        moved = v - middle(check, level)
         resid = moved + total + a_c[level] * v + damp_ref[level] * jnp.tanh(v) - force[level]
         out_resid[level] = resid[8:16, :128]
 
@@ -457,7 +469,8 @@
         compiler_params=small,
     )(place_y, corners, from_odd)
     corner_even = swap(corners_b, "gy", 0, 1, False)
-    scratch = [pltpu.VMEM((levels, 24, 256), f32) for _ in range(23)]
+    scratch = [pltpu.VMEM((levels, 2, 40, 128), f32) for _ in range(8)]
+    scratch += [pltpu.VMEM((levels, 24, 256), f32) for _ in range(14)]
     return tuple(
         pl.pallas_call(
             solve_kernel,

time: 59.4 us -> 59.3 us (level)
  no operation moved by 1% of the time
where the time goes in v4:
time: 59.3 us; the launch traced here: 58.7 us
  starting transfers between devices  34.3 us (58%)
  waiting for transfers between devices  12.9 us (22%)
  Pallas kernels  9.89 us (17%)
  between operations  1.41 us (2%)
    ppermute x6, starting transfers between devices, swap(): return lax.ppermute(array, axis, pairs)  34.3 us
    ppermute x6, waiting for transfers between devices, swap(): return lax.ppermute(array, axis, pairs)  12.9 us
    pallas_call x1, Pallas kernels, compute(): pl.pallas_call(solve_kernel, in_specs=[smem, smem, smem] + vmem(10), out_...  8.38 us
    pallas_call x1, Pallas kernels, compute(): pl.pallas_call(functools.partial(pack_kernel, size_y), in_specs=[smem, sm...  1.45 us
  transfers between devices with their start and end apart: 6, of which 3 were waited for; matrix products, arithmetic and copies ran while one was open for 0% of the time, Pallas kernels for 0%

profile of v4, /device:TPU:6, one launch (start us, length us, event | category | flops | bytes accessed | tf_op | source)
XLA Modules:
  0.0 58.7 jit_solution(5910120847493125389)
XLA Ops:
  0.6 1.4 %shard_map.148 = (f32[8,16,8,128]{3,2,1,0:T(8,128)S(1)}, f32[6,16,8,128]{3,2,1,0:T(8,128)S(1)}, f32[9,8,128]{2,1,0:T(8,128)S(1)}, f32[9,8,128]{2,1,0:T(8,128)S(1)}) custom-call(s32[1]{0:T(128)} %bitcast.2.x_ref, s32[1]{0:T(128)} %bitcast.y_ref, f32[16,8,128]{2,1,0:T(8,128)} %refs_0_.1, f32[16,8,128]{2,1,0:T(8,128)} %refs_1_.1, f32[16,8,128]{2,1,0:T(8,128)} %refs_2_.1, ...), custom_call_target="tpu_custom_call" | custom-call | tf_op jit(solution)/shard_map/pallas_call | solution.py:425
  2.1 1.9 %collective-permute-start.1 = (f32[8,16,8,128]{3,2,1,0:T(8,128)S(1)}, f32[8,16,8,128]{3,2,1,0:T(8,128)S(1)}, u32[]{:S(2)}, u32[]{:S(2)}) collective-permute-start(f32[8,16,8,128]{3,2,1,0:T(8,128)S(1)} %get-tuple-element.9.block.own), channel_id=1, source_target_pairs={{0,1},{1,0},{2,3},{3,2},{4,5},{5,4},{6,7},{7,6},{8,9},{9,8},{10,11... | collective-permute-start | bytes 1572872 | tf_op jit(solution)/shard_map/ppermute | solution.py:389
  4.0 8.3 %collective-permute-start = (f32[6,16,8,128]{3,2,1,0:T(8,128)S(1)}, f32[6,16,8,128]{3,2,1,0:T(8,128)S(1)}, u32[]{:S(2)}, u32[]{:S(2)}) collective-permute-start(f32[6,16,8,128]{3,2,1,0:T(8,128)S(1)} %get-tuple-element.10), channel_id=1, source_target_pairs={{1,2},{2,1},{3,4},{4,3},{5,6},{6,5},{7,8},{8,7},{9,10},{10,9},{11,... | collective-permute-start | bytes 1179656 | tf_op jit(solution)/shard_map/ppermute | solution.py:389
  12.3 18.4 %collective-permute-start.2 = (f32[9,8,128]{2,1,0:T(8,128)S(1)}, f32[9,8,128]{2,1,0:T(8,128)S(1)}, u32[]{:S(2)}, u32[]{:S(2)}) collective-permute-start(f32[9,8,128]{2,1,0:T(8,128)S(1)} %get-tuple-element.11), channel_id=1, source_target_pairs={{32,64},{64,32},{96,128},{128,96},{160,192},{192,160},{224,256},{2... | collective-permute-start | bytes 110600 | tf_op jit(solution)/shard_map/ppermute | solution.py:389
  30.7 1.9 %collective-permute-start.3 = (f32[9,8,128]{2,1,0:T(8,128)S(1)}, f32[9,8,128]{2,1,0:T(8,128)S(1)}, u32[]{:S(2)}, u32[]{:S(2)}) collective-permute-start(f32[9,8,128]{2,1,0:T(8,128)S(1)} %get-tuple-element.12), channel_id=1, source_target_pairs={{0,32},{32,0},{64,96},{96,64},{128,160},{160,128},{192,224},{224,1... | collective-permute-start | bytes 110600 | tf_op jit(solution)/shard_map/ppermute | solution.py:389
  32.6 5.6 %collective-permute-done.2.from_odd = f32[9,8,128]{2,1,0:T(8,128)S(1)} collective-permute-done((f32[9,8,128]{2,1,0:T(8,128)S(1)}, f32[9,8,128]{2,1,0:T(8,128)S(1)}, u32[]{:S(2)}, u32[]{:S(2)}) %collective-permute-start.2) | collective-permute-done | bytes 36896 | tf_op jit(solution)/shard_map/ppermute | solution.py:389
  38.2 0.0 collective-permute-done.3.from_even
  38.2 0.0 collective-permute-done.1.block_even.from_even
  38.3 1.9 %collective-permute-start.4 = (f32[54,8,128]{2,1,0:T(8,128)S(1)}, f32[54,8,128]{2,1,0:T(8,128)S(1)}, u32[]{:S(2)}, u32[]{:S(2)}) collective-permute-start(f32[54,8,128]{2,1,0:T(8,128)S(1)} %get-tuple-element.13.corner_own), channel_id=1, source_target_pairs={{1,2},{2,1},{3,4},{4,3},{5,6},{6,5},{7,8},{8,7},{9,10},{10,9},{11,... | collective-permute-start | bytes 663560 | tf_op jit(solution)/shard_map/ppermute | solution.py:389
  40.8 0.0 copy-start
  40.9 0.0 copy-start.1
  40.9 0.0 collective-permute-done.block_odd.from_odd
  40.9 1.9 %collective-permute-start.5 = (f32[22,8,128]{2,1,0:T(8,128)S(1)}, f32[22,8,128]{2,1,0:T(8,128)S(1)}, u32[]{:S(2)}, u32[]{:S(2)}) collective-permute-start(f32[22,8,128]{2,1,0:T(8,128)S(1)} %shard_map.150), channel_id=1, source_target_pairs={{0,1},{1,0},{2,3},{3,2},{4,5},{5,4},{6,7},{7,6},{8,9},{9,8},{10,11... | collective-permute-start | bytes 270344 | tf_op jit(solution)/shard_map/ppermute | solution.py:389
  42.8 0.1 fusion.4.cos_ref
  42.9 0.0 copy-start.2
  42.9 0.0 copy-start.3
  42.9 1.2 %collective-permute-done.5.corner_even = f32[22,8,128]{2,1,0:T(8,128)S(1)} collective-permute-done((f32[22,8,128]{2,1,0:T(8,128)S(1)}, f32[22,8,128]{2,1,0:T(8,128)S(1)}, u32[]{:S(2)}, u32[]{:S(2)}) %collective-permute-start.5) | collective-permute-done | bytes 90144 | tf_op jit(solution)/shard_map/ppermute | solution.py:389
  44.1 6.2 %collective-permute-done.4.corner_odd = f32[54,8,128]{2,1,0:T(8,128)S(1)} collective-permute-done((f32[54,8,128]{2,1,0:T(8,128)S(1)}, f32[54,8,128]{2,1,0:T(8,128)S(1)}, u32[]{:S(2)}, u32[]{:S(2)}) %collective-permute-start.4) | collective-permute-done | bytes 221216 | tf_op jit(solution)/shard_map/ppermute | solution.py:389
  50.3 0.0 copy-done
  50.3 0.0 copy-done.1
  50.3 0.0 copy-done.2
  50.3 0.0 copy-done.3
  50.3 8.4 %shard_map.151 = (f32[16,8,128]{2,1,0:T(8,128)}, f32[16,8,128]{2,1,0:T(8,128)}, f32[16,8,128]{2,1,0:T(8,128)}) custom-call(s32[1]{0:T(128)} %bitcast.y_ref, f32[16]{0:T(128)S(1)} %copy-done.2, f32[16]{0:T(128)S(1)} %copy-done.3, f32[1,256]{1,0:T(1,128)S(1)} %fusion.4.cos_ref, f32[8,16,8,128]{3,2,1,0:T(8,128)S(1)} %get-tuple-element.9.block.own, ...), custom_call_target="tpu_custom_call" | custom-call | tf_op jit(solution)/shard_map/pallas_call | solution.py:475
  (2 shorter events, 0.1 us)
Async XLA Ops:
  2.1 36.1 %collective-permute-start.1 = (f32[8,16,8,128]{3,2,1,0:T(8,128)S(1)}, f32[8,16,8,128]{3,2,1,0:T(8,128)S(1)}, u32[]{:S(2)}, u32[]{:S(2)}) collective-permute-start(f32[8,16,8,128]{3,2,1,0:T(8,128)S(1)} %get-tuple-element.9.block.own), channel_id=1, source_target_pairs={{0,1},{1,0},{2,3},{3,2},{4,5},{5,4},{6,7},{7,6},{8,9},{9,8},{10,11... | collective-permute-start | bytes 1572872 | tf_op jit(solution)/shard_map/ppermute | solution.py:389
  4.0 36.8 %collective-permute-start = (f32[6,16,8,128]{3,2,1,0:T(8,128)S(1)}, f32[6,16,8,128]{3,2,1,0:T(8,128)S(1)}, u32[]{:S(2)}, u32[]{:S(2)}) collective-permute-start(f32[6,16,8,128]{3,2,1,0:T(8,128)S(1)} %get-tuple-element.10), channel_id=1, source_target_pairs={{1,2},{2,1},{3,4},{4,3},{5,6},{6,5},{7,8},{8,7},{9,10},{10,9},{11,... | collective-permute-start | bytes 1179656 | tf_op jit(solution)/shard_map/ppermute | solution.py:389
  12.3 25.9 %collective-permute-start.2 = (f32[9,8,128]{2,1,0:T(8,128)S(1)}, f32[9,8,128]{2,1,0:T(8,128)S(1)}, u32[]{:S(2)}, u32[]{:S(2)}) collective-permute-start(f32[9,8,128]{2,1,0:T(8,128)S(1)} %get-tuple-element.11), channel_id=1, source_target_pairs={{32,64},{64,32},{96,128},{128,96},{160,192},{192,160},{224,256},{2... | collective-permute-start | bytes 110600 | tf_op jit(solution)/shard_map/ppermute | solution.py:389
  30.7 7.5 %collective-permute-start.3 = (f32[9,8,128]{2,1,0:T(8,128)S(1)}, f32[9,8,128]{2,1,0:T(8,128)S(1)}, u32[]{:S(2)}, u32[]{:S(2)}) collective-permute-start(f32[9,8,128]{2,1,0:T(8,128)S(1)} %get-tuple-element.12), channel_id=1, source_target_pairs={{0,32},{32,0},{64,96},{96,64},{128,160},{160,128},{192,224},{224,1... | collective-permute-start | bytes 110600 | tf_op jit(solution)/shard_map/ppermute | solution.py:389
  38.3 12.0 %collective-permute-start.4 = (f32[54,8,128]{2,1,0:T(8,128)S(1)}, f32[54,8,128]{2,1,0:T(8,128)S(1)}, u32[]{:S(2)}, u32[]{:S(2)}) collective-permute-start(f32[54,8,128]{2,1,0:T(8,128)S(1)} %get-tuple-element.13.corner_own), channel_id=1, source_target_pairs={{1,2},{2,1},{3,4},{4,3},{5,6},{6,5},{7,8},{8,7},{9,10},{10,9},{11,... | collective-permute-start | bytes 663560 | tf_op jit(solution)/shard_map/ppermute | solution.py:389
  40.8 9.4 %copy-start = (f32[16,8,128]{2,1,0:T(8,128)S(1)}, f32[16,8,128]{2,1,0:T(8,128)}, u32[]{:S(2)}) copy-start(f32[16,8,128]{2,1,0:T(8,128)} %observations.1) | copy-start | bytes 196612
  40.9 9.4 %copy-start.1 = (f32[16,8,128]{2,1,0:T(8,128)S(1)}, f32[16,8,128]{2,1,0:T(8,128)}, u32[]{:S(2)}) copy-start(f32[16,8,128]{2,1,0:T(8,128)} %weight.1) | copy-start | bytes 196612
  40.9 3.2 %collective-permute-start.5 = (f32[22,8,128]{2,1,0:T(8,128)S(1)}, f32[22,8,128]{2,1,0:T(8,128)S(1)}, u32[]{:S(2)}, u32[]{:S(2)}) collective-permute-start(f32[22,8,128]{2,1,0:T(8,128)S(1)} %shard_map.150), channel_id=1, source_target_pairs={{0,1},{1,0},{2,3},{3,2},{4,5},{5,4},{6,7},{7,6},{8,9},{9,8},{10,11... | collective-permute-start | bytes 270344 | tf_op jit(solution)/shard_map/ppermute | solution.py:389
  42.9 7.4 %copy-start.2 = (f32[16]{0:T(128)S(1)}, f32[16]{0:T(128)}, u32[]{:S(2)}) copy-start(f32[16]{0:T(128)} %level_ref.1) | copy-start | bytes 196
  42.9 7.4 %copy-start.3 = (f32[16]{0:T(128)S(1)}, f32[16]{0:T(128)}, u32[]{:S(2)}) copy-start(f32[16]{0:T(128)} %damp_ref.1) | copy-start | bytes 196

commit v5 on v4

--- a/solution.py
+++ b/solution.py
@@ -72,12 +72,13 @@
         corners[levels + row // 8, at : at + 1] = line
 
 
-def corner_odd_kernel(x_ref, y_ref, from_odd, from_even, block_even, block, corners, rims):
+def corner_odd_kernel(x_ref, y_ref, from_odd, from_even, block_even, block, corners, rims, parity):
     half = from_odd.shape[0] - 1
     odd_x = x_ref[0] % 2 == 1
     for place in range(half):
         corners[place] = jnp.where(odd_x, from_even[place], from_odd[place])
         corners[half + place] = jnp.where(odd_x, from_odd[place], from_even[place])
+    parity[...] = jnp.where(y_ref[0] % 2 == 1, 1.0, jnp.zeros((8, 128), jnp.float32))
     rims[0] = jnp.where(odd_x, from_even[half], from_odd[half])
     rims[1] = jnp.where(odd_x, from_odd[half], from_even[half])
     relay(y_ref[0] % 2 == 1, True, block_even, corners)
@@ -88,17 +89,19 @@
             corners[base + (k - FORWARD) * levels + level] = block[k, level]
 
 
-def corner_even_kernel(y_ref, corner_own, block_odd, corners):
+def corner_even_kernel(y_ref, level_ref, damp_ref, corner_own, block_odd, corners, table):
+    for level in range(block_odd.shape[1]):
+        table[0, level] = level_ref[level]
+        table[1, level] = damp_ref[level]
     for place in range(block_odd.shape[1]):
         corners[place] = corner_own[place]
     relay(y_ref[0] % 2 == 1, False, block_odd, corners)
 
 
 def solve_kernel(
-    y_ref,
-    level_ref,
-    damp_ref,
+    table,
     cos_ref,
+    parity,
     own,
     from_odd,
     from_even,
@@ -138,7 +141,7 @@
     lanes = lane_ids()
 
     half = levels // 2
-    odd_y = y_ref[0] % 2 == 1
+    odd_y = parity[...] > 0.5
 
     def odd_tile(k, at):
         if k < FORWARD:
@@ -222,10 +225,10 @@
         return pltpu.roll(v, 1, 1)
 
     def up(level):
-        return level_ref[level] if level < levels - 1 else None
+        return table[0, level] if level < levels - 1 else None
 
     def down(level):
-        return level_ref[level - 1] if level > 0 else None
+        return table[0, level - 1] if level > 0 else None
 
     def pair(level):
         parts = [u for u in (up(level), down(level)) if u is not None]
@@ -258,11 +261,13 @@
             below, here = here, above
 
     blank = jnp.zeros((8, 128), jnp.float32)
-    for ref in (check, d, x, d_a, mu, up_n, low_n, north):
-        for level in range(levels):
-            for side in range(2):
+    for level in range(levels):
+        for ref in (check, d, x, d_a, mu, up_n, low_n, north):
+            faces = any(ref is face for face in (up_n, low_n, north))
+            for side in (1,) if faces or ref is check else (0, 1):
                 ref[level, side, 0:8] = blank
-                ref[level, side, 32:40] = blank
+                if not faces:
+                    ref[level, side, 32:40] = blank
 
     for level in range(levels):
         pairs = strips(level)
@@ -293,7 +298,7 @@
         check[level, 0, 32:33] = far_north(level)
         force[level] = gather(S, level, pairs) * cos_ref[...]
         tangent = jnp.tanh(gather(TR, level, pairs))
-        local = damp_ref[level] * (1.0 - tangent * tangent)
+        local = table[1, level] * (1.0 - tangent * tangent)
         weight_a = RELAXATION / (base + local)
         af = gather(AF, level, pairs)
         diagonal = 1.0 + center + local
@@ -305,7 +310,7 @@
         keep(d_a, level, start)
 
     def newton(level, resid, tangent):
-        local = damp_ref[level] * (1.0 - tangent * tangent)
+        local = table[1, level] * (1.0 - tangent * tangent)
         w = RELAXATION / (diag[level] + local)
         wt[level] = w
         ctr[level] = 1.0 - w * (1.0 + a_c[level] + local)
@@ -316,7 +321,7 @@
     def first_resid(field, level, v, below, above):
         tangent = jnp.tanh(v)
         total = forward_sum(field, level, v, below, above)
-        resid = total + a_c[level] * v + damp_ref[level] * tangent - force[level]
+        resid = total + a_c[level] * v + table[1, level] * tangent - force[level]
         newton(level, resid, tangent)
 
     def forward_lin(field, level, v, below, above):
@@ -345,7 +350,7 @@
         tangent = jnp.tanh(v)
         total = forward_sum(field, level, v, below, above)
         moved = v - middle(check, level)
-        resid = moved + total + a_c[level] * v + damp_ref[level] * tangent - force[level]
+        resid = moved + total + a_c[level] * v + table[1, level] * tangent - force[level]
         newton(level, resid, tangent)
 
     def adjoint_resid(field, level, v, below, above):
@@ -369,7 +374,7 @@
     def final_resid(field, level, v, below, above):
         total = forward_sum(field, level, v, below, above)
         moved = v - middle(check, level)
-        resid = moved + total + a_c[level] * v + damp_ref[level] * jnp.tanh(v) - force[level]
+        resid = moved + total + a_c[level] * v + table[1, level] * jnp.tanh(v) - force[level]
         out_resid[level] = resid[8:16, :128]
 
     sweep(x, final_resid)
@@ -450,40 +455,40 @@
     lon_even = swap(strip_even, "gx", 0, 1, True)
     corner_shape = (levels + 3 * levels // 8, lat_rows, lon_cols)
     small = pltpu.CompilerParams(vmem_limit_bytes=4 * 1024 * 1024)
-    corners, rims = pl.pallas_call(
+    corners, rims, parity = pl.pallas_call(
         corner_odd_kernel,
         in_specs=[smem, smem] + vmem(4),
-        out_specs=vmem(2),
+        out_specs=vmem(3),
         out_shape=[
             pltpu.VMEM((corner_shape[0] + 2 * levels,) + corner_shape[1:], f32),
             pltpu.VMEM((2, lat_rows, lon_cols), f32),
+            pltpu.VMEM((lat_rows, lon_cols), f32),
         ],
         compiler_params=small,
     )(place_x, place_y, lon_odd, lon_even, from_even, block)
     corner_odd = swap(corners, "gy", 1, 1, False)
-    corners_b = pl.pallas_call(
+    corners_b, table = pl.pallas_call(
         corner_even_kernel,
-        in_specs=[smem] + vmem(2),
-        out_specs=vmem(1)[0],
-        out_shape=pltpu.VMEM(corner_shape, f32),
+        in_specs=[smem] * 3 + vmem(2),
+        out_specs=[vmem(1)[0], smem],
+        out_shape=[pltpu.VMEM(corner_shape, f32), pltpu.SMEM((2, levels), f32)],
         compiler_params=small,
-    )(place_y, corners, from_odd)
+    )(place_y, level_diffusion, damping, corners, from_odd)
     corner_even = swap(corners_b, "gy", 0, 1, False)
     scratch = [pltpu.VMEM((levels, 2, 40, 128), f32) for _ in range(8)]
     scratch += [pltpu.VMEM((levels, 24, 256), f32) for _ in range(14)]
     return tuple(
         pl.pallas_call(
             solve_kernel,
-            in_specs=[smem, smem, smem] + vmem(10),
+            in_specs=[smem] + vmem(11),
             out_specs=vmem(3),
             out_shape=[jax.ShapeDtypeStruct(tile, f32)] * 3,
             scratch_shapes=scratch,
             compiler_params=pltpu.CompilerParams(vmem_limit_bytes=20 * 1024 * 1024),
         )(
-            place_y,
-            level_diffusion,
-            damping,
+            table,
             wave,
+            parity,
             block,
             from_odd,
             from_even,

time: 59.3 us -> 58.9 us (level)
  waiting for transfers between devices: 12.9 us -> 11.8 us
  local copies, waits for them, and re-layouts: 0.03 us -> 0.63 us
    ppermute x6, waiting for transfers between devices: 12.9 us -> 11.8 us  [swap(): return lax.ppermute(array, axis, pairs)]
    unnamed x8, local copies, waits for them, and re-layouts: 0.03 us -> 0.63 us
  transfers between devices with their start and end apart: 6 -> 6, of which waited for: 3 -> 3; matrix products, arithmetic and copies ran while one was open for 0% -> 0% of each run, Pallas kernels for 0% -> 1%
where the time goes in v5:
time: 58.9 us; the launch traced here: 58.2 us
  starting transfers between devices  34.3 us (58%)
  waiting for transfers between devices  11.8 us (20%)
  Pallas kernels  10 us (17%)
  between operations  1.4 us (2%)
  local copies, waits for them, and re-layouts  0.63 us (1%)
    ppermute x6, starting transfers between devices, swap(): return lax.ppermute(array, axis, pairs)  34.3 us
    ppermute x6, waiting for transfers between devices, swap(): return lax.ppermute(array, axis, pairs)  11.8 us
    pallas_call x1, Pallas kernels, compute(): pl.pallas_call(solve_kernel, in_specs=[smem] + vmem(11), out_specs=vmem(3...  7.94 us
    pallas_call x1, Pallas kernels, compute(): pl.pallas_call(functools.partial(pack_kernel, size_y), in_specs=[smem, sm...  1.45 us
  transfers between devices with their start and end apart: 6, of which 3 were waited for; matrix products, arithmetic and copies ran while one was open for 0% of the time, Pallas kernels for 1%

profile of v5, /device:TPU:6, one launch (start us, length us, event | category | flops | bytes accessed | tf_op | source)
XLA Modules:
  0.0 58.2 jit_solution(2978712953148058483)
XLA Ops:
  0.6 1.5 %shard_map.148 = (f32[8,16,8,128]{3,2,1,0:T(8,128)S(1)}, f32[6,16,8,128]{3,2,1,0:T(8,128)S(1)}, f32[9,8,128]{2,1,0:T(8,128)S(1)}, f32[9,8,128]{2,1,0:T(8,128)S(1)}) custom-call(s32[1]{0:T(128)} %bitcast.1.x_ref, s32[1]{0:T(128)} %bitcast.y_ref, f32[16,8,128]{2,1,0:T(8,128)} %refs_0_.1, f32[16,8,128]{2,1,0:T(8,128)} %refs_1_.1, f32[16,8,128]{2,1,0:T(8,128)} %refs_2_.1, ...), custom_call_target="tpu_custom_call" | custom-call | tf_op jit(solution)/shard_map/pallas_call | solution.py:430
  2.1 1.9 %collective-permute-start.2 = (f32[8,16,8,128]{3,2,1,0:T(8,128)S(1)}, f32[8,16,8,128]{3,2,1,0:T(8,128)S(1)}, u32[]{:S(2)}, u32[]{:S(2)}) collective-permute-start(f32[8,16,8,128]{3,2,1,0:T(8,128)S(1)} %get-tuple-element.14.block.own), channel_id=1, source_target_pairs={{0,1},{1,0},{2,3},{3,2},{4,5},{5,4},{6,7},{7,6},{8,9},{9,8},{10,11... | collective-permute-start | bytes 1572872 | tf_op jit(solution)/shard_map/ppermute | solution.py:394
  4.0 8.3 %collective-permute-start.3 = (f32[6,16,8,128]{3,2,1,0:T(8,128)S(1)}, f32[6,16,8,128]{3,2,1,0:T(8,128)S(1)}, u32[]{:S(2)}, u32[]{:S(2)}) collective-permute-start(f32[6,16,8,128]{3,2,1,0:T(8,128)S(1)} %get-tuple-element.16), channel_id=1, source_target_pairs={{1,2},{2,1},{3,4},{4,3},{5,6},{6,5},{7,8},{8,7},{9,10},{10,9},{11,... | collective-permute-start | bytes 1179656 | tf_op jit(solution)/shard_map/ppermute | solution.py:394
  12.3 18.4 %collective-permute-start = (f32[9,8,128]{2,1,0:T(8,128)S(1)}, f32[9,8,128]{2,1,0:T(8,128)S(1)}, u32[]{:S(2)}, u32[]{:S(2)}) collective-permute-start(f32[9,8,128]{2,1,0:T(8,128)S(1)} %get-tuple-element.12), channel_id=1, source_target_pairs={{32,64},{64,32},{96,128},{128,96},{160,192},{192,160},{224,256},{2... | collective-permute-start | bytes 110600 | tf_op jit(solution)/shard_map/ppermute | solution.py:394
  30.7 1.9 %collective-permute-start.1 = (f32[9,8,128]{2,1,0:T(8,128)S(1)}, f32[9,8,128]{2,1,0:T(8,128)S(1)}, u32[]{:S(2)}, u32[]{:S(2)}) collective-permute-start(f32[9,8,128]{2,1,0:T(8,128)S(1)} %get-tuple-element.13), channel_id=1, source_target_pairs={{0,32},{32,0},{64,96},{96,64},{128,160},{160,128},{192,224},{224,1... | collective-permute-start | bytes 110600 | tf_op jit(solution)/shard_map/ppermute | solution.py:394
  32.6 5.6 %collective-permute-done.from_odd = f32[9,8,128]{2,1,0:T(8,128)S(1)} collective-permute-done((f32[9,8,128]{2,1,0:T(8,128)S(1)}, f32[9,8,128]{2,1,0:T(8,128)S(1)}, u32[]{:S(2)}, u32[]{:S(2)}) %collective-permute-start) | collective-permute-done | bytes 36896 | tf_op jit(solution)/shard_map/ppermute | solution.py:394
  38.2 0.0 collective-permute-done.1.from_even
  38.2 0.0 collective-permute-done.2.block_even.from_even
  38.3 1.9 %collective-permute-start.4 = (f32[54,8,128]{2,1,0:T(8,128)S(1)}, f32[54,8,128]{2,1,0:T(8,128)S(1)}, u32[]{:S(2)}, u32[]{:S(2)}) collective-permute-start(f32[54,8,128]{2,1,0:T(8,128)S(1)} %get-tuple-element.15.corner_own), channel_id=1, source_target_pairs={{1,2},{2,1},{3,4},{4,3},{5,6},{6,5},{7,8},{8,7},{9,10},{10,9},{11,... | collective-permute-start | bytes 663560 | tf_op jit(solution)/shard_map/ppermute | solution.py:394
  40.8 0.0 copy-start.2
  40.9 0.0 copy-start.3
  40.9 0.0 copy-start
  40.9 0.0 copy-start.1
  40.9 0.0 collective-permute-done.3.block_odd.from_odd
  40.9 0.6 %copy-done.2 = f32[16]{0:T(128)S(1)} copy-done((f32[16]{0:T(128)S(1)}, f32[16]{0:T(128)}, u32[]{:S(2)}) %copy-start.2) | copy-done | bytes 88
  41.5 0.0 copy-done.3
  41.5 0.6 %shard_map.150 = (f32[22,8,128]{2,1,0:T(8,128)S(1)}, f32[2,16]{1,0:T(2,128)S(4)}) custom-call(s32[1]{0:T(128)} %bitcast.y_ref, f32[16]{0:T(128)S(1)} %copy-done.2, f32[16]{0:T(128)S(1)} %copy-done.3, f32[54,8,128]{2,1,0:T(8,128)S(1)} %get-tuple-element.15.corner_own, f32[6,16,8,128]{3,2,1,0:T(8,128)S(1)} %collective-permute-done.3.block_odd.from_odd), custom_call_target="tpu_custom_call" | custom-call | tf_op jit(solution)/shard_map/pallas_call | solution.py:470
  42.1 1.9 %collective-permute-start.5 = (f32[22,8,128]{2,1,0:T(8,128)S(1)}, f32[22,8,128]{2,1,0:T(8,128)S(1)}, u32[]{:S(2)}, u32[]{:S(2)}) collective-permute-start(f32[22,8,128]{2,1,0:T(8,128)S(1)} %get-tuple-element.19), channel_id=1, source_target_pairs={{0,1},{1,0},{2,3},{3,2},{4,5},{5,4},{6,7},{7,6},{8,9},{9,8},{10,11... | collective-permute-start | bytes 270344 | tf_op jit(solution)/shard_map/ppermute | solution.py:394
  44.0 0.1 fusion.4.cos_ref
  44.1 1.2 %collective-permute-done.5.corner_even = f32[22,8,128]{2,1,0:T(8,128)S(1)} collective-permute-done((f32[22,8,128]{2,1,0:T(8,128)S(1)}, f32[22,8,128]{2,1,0:T(8,128)S(1)}, u32[]{:S(2)}, u32[]{:S(2)}) %collective-permute-start.5) | collective-permute-done | bytes 90144 | tf_op jit(solution)/shard_map/ppermute | solution.py:394
  45.3 5.0 %collective-permute-done.4.corner_odd = f32[54,8,128]{2,1,0:T(8,128)S(1)} collective-permute-done((f32[54,8,128]{2,1,0:T(8,128)S(1)}, f32[54,8,128]{2,1,0:T(8,128)S(1)}, u32[]{:S(2)}, u32[]{:S(2)}) %collective-permute-start.4) | collective-permute-done | bytes 221216 | tf_op jit(solution)/shard_map/ppermute | solution.py:394
  50.3 0.0 copy-done
  50.3 0.0 copy-done.1
  50.3 7.9 %shard_map.151 = (f32[16,8,128]{2,1,0:T(8,128)}, f32[16,8,128]{2,1,0:T(8,128)}, f32[16,8,128]{2,1,0:T(8,128)}) custom-call(f32[2,16]{1,0:T(2,128)S(4)} %get-tuple-element.17.table, f32[1,256]{1,0:T(1,128)S(1)} %fusion.4.cos_ref, f32[8,128]{1,0:T(8,128)S(1)} %get-tuple-element.18.parity, f32[8,16,8,128]{3,2,1,0:T(8,128)S(1)} %get-tuple-element.14.block.own, ...), custom_call_target="tpu_custom_call" | custom-call | tf_op jit(solution)/shard_map/pallas_call | solution.py:481
  (1 shorter events, 0.0 us)
Async XLA Ops:
  2.1 36.1 %collective-permute-start.2 = (f32[8,16,8,128]{3,2,1,0:T(8,128)S(1)}, f32[8,16,8,128]{3,2,1,0:T(8,128)S(1)}, u32[]{:S(2)}, u32[]{:S(2)}) collective-permute-start(f32[8,16,8,128]{3,2,1,0:T(8,128)S(1)} %get-tuple-element.14.block.own), channel_id=1, source_target_pairs={{0,1},{1,0},{2,3},{3,2},{4,5},{5,4},{6,7},{7,6},{8,9},{9,8},{10,11... | collective-permute-start | bytes 1572872 | tf_op jit(solution)/shard_map/ppermute | solution.py:394
  4.0 36.9 %collective-permute-start.3 = (f32[6,16,8,128]{3,2,1,0:T(8,128)S(1)}, f32[6,16,8,128]{3,2,1,0:T(8,128)S(1)}, u32[]{:S(2)}, u32[]{:S(2)}) collective-permute-start(f32[6,16,8,128]{3,2,1,0:T(8,128)S(1)} %get-tuple-element.16), channel_id=1, source_target_pairs={{1,2},{2,1},{3,4},{4,3},{5,6},{6,5},{7,8},{8,7},{9,10},{10,9},{11,... | collective-permute-start | bytes 1179656 | tf_op jit(solution)/shard_map/ppermute | solution.py:394
  12.3 25.9 %collective-permute-start = (f32[9,8,128]{2,1,0:T(8,128)S(1)}, f32[9,8,128]{2,1,0:T(8,128)S(1)}, u32[]{:S(2)}, u32[]{:S(2)}) collective-permute-start(f32[9,8,128]{2,1,0:T(8,128)S(1)} %get-tuple-element.12), channel_id=1, source_target_pairs={{32,64},{64,32},{96,128},{128,96},{160,192},{192,160},{224,256},{2... | collective-permute-start | bytes 110600 | tf_op jit(solution)/shard_map/ppermute | solution.py:394
  30.7 7.5 %collective-permute-start.1 = (f32[9,8,128]{2,1,0:T(8,128)S(1)}, f32[9,8,128]{2,1,0:T(8,128)S(1)}, u32[]{:S(2)}, u32[]{:S(2)}) collective-permute-start(f32[9,8,128]{2,1,0:T(8,128)S(1)} %get-tuple-element.13), channel_id=1, source_target_pairs={{0,32},{32,0},{64,96},{96,64},{128,160},{160,128},{192,224},{224,1... | collective-permute-start | bytes 110600 | tf_op jit(solution)/shard_map/ppermute | solution.py:394
  38.3 12.0 %collective-permute-start.4 = (f32[54,8,128]{2,1,0:T(8,128)S(1)}, f32[54,8,128]{2,1,0:T(8,128)S(1)}, u32[]{:S(2)}, u32[]{:S(2)}) collective-permute-start(f32[54,8,128]{2,1,0:T(8,128)S(1)} %get-tuple-element.15.corner_own), channel_id=1, source_target_pairs={{1,2},{2,1},{3,4},{4,3},{5,6},{6,5},{7,8},{8,7},{9,10},{10,9},{11,... | collective-permute-start | bytes 663560 | tf_op jit(solution)/shard_map/ppermute | solution.py:394
  40.8 0.7 %copy-start.2 = (f32[16]{0:T(128)S(1)}, f32[16]{0:T(128)}, u32[]{:S(2)}) copy-start(f32[16]{0:T(128)} %level_ref.1) | copy-start | bytes 196
  40.9 0.7 %copy-start.3 = (f32[16]{0:T(128)S(1)}, f32[16]{0:T(128)}, u32[]{:S(2)}) copy-start(f32[16]{0:T(128)} %damp_ref.1) | copy-start | bytes 196
  40.9 9.4 %copy-start = (f32[16,8,128]{2,1,0:T(8,128)S(1)}, f32[16,8,128]{2,1,0:T(8,128)}, u32[]{:S(2)}) copy-start(f32[16,8,128]{2,1,0:T(8,128)} %observations.1) | copy-start | bytes 196612
  40.9 9.4 %copy-start.1 = (f32[16,8,128]{2,1,0:T(8,128)S(1)}, f32[16,8,128]{2,1,0:T(8,128)}, u32[]{:S(2)}) copy-start(f32[16,8,128]{2,1,0:T(8,128)} %weight.1) | copy-start | bytes 196612
  42.1 3.2 %collective-permute-start.5 = (f32[22,8,128]{2,1,0:T(8,128)S(1)}, f32[22,8,128]{2,1,0:T(8,128)S(1)}, u32[]{:S(2)}, u32[]{:S(2)}) collective-permute-start(f32[22,8,128]{2,1,0:T(8,128)S(1)} %get-tuple-element.19), channel_id=1, source_target_pairs={{0,1},{1,0},{2,3},{3,2},{4,5},{5,4},{6,7},{7,6},{8,9},{9,8},{10,11... | collective-permute-start | bytes 270344 | tf_op jit(solution)/shard_map/ppermute | solution.py:394

commit v6 on v5

--- a/solution.py
+++ b/solution.py
@@ -24,9 +24,12 @@
     return value if shift % 128 == 0 else pltpu.roll(value, shift % 128, 1)
 
 
-def pack_kernel(size_y, x_ref, y_ref, *refs):
+def pack_kernel(size_y, x_ref, y_ref, level_ref, damp_ref, *refs):
     fields = refs[:FIELDS]
-    block, block_f, strip_odd, strip_even = refs[FIELDS:]
+    block, block_f, strip_odd, strip_even, table = refs[FIELDS:]
+    for level in range(fields[0].shape[0]):
+        table[0, level] = level_ref[level]
+        table[1, level] = damp_ref[level]
     odd_x, last = x_ref[0] % 2 == 1, y_ref[0] == size_y - 1
     levels = fields[0].shape[0]
     half = levels // 2
@@ -89,10 +92,7 @@
             corners[base + (k - FORWARD) * levels + level] = block[k, level]
 
 
-def corner_even_kernel(y_ref, level_ref, damp_ref, corner_own, block_odd, corners, table):
-    for level in range(block_odd.shape[1]):
-        table[0, level] = level_ref[level]
-        table[1, level] = damp_ref[level]
+def corner_even_kernel(y_ref, corner_own, block_odd, corners):
     for place in range(block_odd.shape[1]):
         corners[place] = corner_own[place]
     relay(y_ref[0] % 2 == 1, False, block_odd, corners)
@@ -427,19 +427,22 @@
     f32 = jnp.float32
     smem = pl.BlockSpec(memory_space=pltpu.SMEM)
     strip = (levels // 2 + 1, lat_rows, lon_cols)
-    block, block_f, strip_odd, strip_even = pl.pallas_call(
+    block, block_f, strip_odd, strip_even, table = pl.pallas_call(
         functools.partial(pack_kernel, size_y),
-        in_specs=[smem, smem] + vmem(8),
-        out_specs=vmem(4),
+        in_specs=[smem] * 4 + vmem(8),
+        out_specs=vmem(4) + [smem],
         out_shape=[
             pltpu.VMEM((FIELDS,) + tile, f32),
             pltpu.VMEM((FORWARD,) + tile, f32),
             pltpu.VMEM(strip, f32),
             pltpu.VMEM(strip, f32),
+            pltpu.SMEM((2, levels), f32),
         ],
     )(
         place_x,
         place_y,
+        level_diffusion,
+        damping,
         checkpoint,
         source,
         east_diffusion,
@@ -467,13 +470,13 @@
         compiler_params=small,
     )(place_x, place_y, lon_odd, lon_even, from_even, block)
     corner_odd = swap(corners, "gy", 1, 1, False)
-    corners_b, table = pl.pallas_call(
+    corners_b = pl.pallas_call(
         corner_even_kernel,
-        in_specs=[smem] * 3 + vmem(2),
-        out_specs=[vmem(1)[0], smem],
-        out_shape=[pltpu.VMEM(corner_shape, f32), pltpu.SMEM((2, levels), f32)],
+        in_specs=[smem] + vmem(2),
+        out_specs=vmem(1)[0],
+        out_shape=pltpu.VMEM(corner_shape, f32),
         compiler_params=small,
-    )(place_y, level_diffusion, damping, corners, from_odd)
+    )(place_y, corners, from_odd)
     corner_even = swap(corners_b, "gy", 0, 1, False)
     scratch = [pltpu.VMEM((levels, 2, 40, 128), f32) for _ in range(8)]
     scratch += [pltpu.VMEM((levels, 24, 256), f32) for _ in range(14)]

time: 58.9 us -> 58.9 us (level)
  waiting for transfers between devices: 11.8 us -> 13 us
  local copies, waits for them, and re-layouts: 0.63 us -> 0.01 us
    ppermute x6, waiting for transfers between devices: 11.8 us -> 13 us  [swap(): return lax.ppermute(array, axis, pairs)]
    unnamed x8 -> x4, local copies, waits for them, and re-layouts: 0.63 us -> 0.01 us
  transfers between devices with their start and end apart: 6 -> 6, of which waited for: 3 -> 3; matrix products, arithmetic and copies ran while one was open for 0% -> 0% of each run, Pallas kernels for 1% -> 0%
where the time goes in v6:
time: 58.9 us; the launch traced here: 58.2 us
  starting transfers between devices  34.3 us (58%)
  waiting for transfers between devices  13 us (22%)
  Pallas kernels  9.47 us (16%)
  between operations  1.39 us (2%)
    ppermute x6, starting transfers between devices, swap(): return lax.ppermute(array, axis, pairs)  34.3 us
    ppermute x6, waiting for transfers between devices, swap(): return lax.ppermute(array, axis, pairs)  13 us
    pallas_call x1, Pallas kernels, compute(): pl.pallas_call(solve_kernel, in_specs=[smem] + vmem(11), out_specs=vmem(3...  7.94 us
    pallas_call x1, Pallas kernels, compute(): pl.pallas_call(functools.partial(pack_kernel, size_y), in_specs=[smem] *...  1.46 us
  transfers between devices with their start and end apart: 6, of which 3 were waited for; matrix products, arithmetic and copies ran while one was open for 0% of the time, Pallas kernels for 0%

profile of v6, /device:TPU:6, one launch (start us, length us, event | category | flops | bytes accessed | tf_op | source)
XLA Modules:
  0.0 58.2 jit_solution(895830870100689197)
XLA Ops:
  0.6 1.5 %shard_map.148 = (f32[8,16,8,128]{3,2,1,0:T(8,128)S(1)}, f32[6,16,8,128]{3,2,1,0:T(8,128)S(1)}, f32[9,8,128]{2,1,0:T(8,128)S(1)}, f32[9,8,128]{2,1,0:T(8,128)S(1)}, f32[2,16]{1,0:T(2,128)S(4)}) custom-call(s32[1]{0:T(128)} %bitcast.x_ref, s32[1]{0:T(128)} %bitcast.1.y_ref, f32[16]{0:T(128)} %level_ref.1, f32[16]{0:T(128)} %damp_ref.1, ...), custom_call_target="tpu_custom_call" | custom-call | tf_op jit(solution)/shard_map/pallas_call | solution.py:430
  2.1 1.9 %collective-permute-start.2 = (f32[8,16,8,128]{3,2,1,0:T(8,128)S(1)}, f32[8,16,8,128]{3,2,1,0:T(8,128)S(1)}, u32[]{:S(2)}, u32[]{:S(2)}) collective-permute-start(f32[8,16,8,128]{3,2,1,0:T(8,128)S(1)} %get-tuple-element.14.block.own), channel_id=1, source_target_pairs={{0,1},{1,0},{2,3},{3,2},{4,5},{5,4},{6,7},{7,6},{8,9},{9,8},{10,11... | collective-permute-start | bytes 1572872 | tf_op jit(solution)/shard_map/ppermute | solution.py:394
  4.0 8.3 %collective-permute-start.3 = (f32[6,16,8,128]{3,2,1,0:T(8,128)S(1)}, f32[6,16,8,128]{3,2,1,0:T(8,128)S(1)}, u32[]{:S(2)}, u32[]{:S(2)}) collective-permute-start(f32[6,16,8,128]{3,2,1,0:T(8,128)S(1)} %get-tuple-element.16), channel_id=1, source_target_pairs={{1,2},{2,1},{3,4},{4,3},{5,6},{6,5},{7,8},{8,7},{9,10},{10,9},{11,... | collective-permute-start | bytes 1179656 | tf_op jit(solution)/shard_map/ppermute | solution.py:394
  12.3 18.4 %collective-permute-start = (f32[9,8,128]{2,1,0:T(8,128)S(1)}, f32[9,8,128]{2,1,0:T(8,128)S(1)}, u32[]{:S(2)}, u32[]{:S(2)}) collective-permute-start(f32[9,8,128]{2,1,0:T(8,128)S(1)} %get-tuple-element.12), channel_id=1, source_target_pairs={{32,64},{64,32},{96,128},{128,96},{160,192},{192,160},{224,256},{2... | collective-permute-start | bytes 110600 | tf_op jit(solution)/shard_map/ppermute | solution.py:394
  30.7 1.9 %collective-permute-start.1 = (f32[9,8,128]{2,1,0:T(8,128)S(1)}, f32[9,8,128]{2,1,0:T(8,128)S(1)}, u32[]{:S(2)}, u32[]{:S(2)}) collective-permute-start(f32[9,8,128]{2,1,0:T(8,128)S(1)} %get-tuple-element.13), channel_id=1, source_target_pairs={{0,32},{32,0},{64,96},{96,64},{128,160},{160,128},{192,224},{224,1... | collective-permute-start | bytes 110600 | tf_op jit(solution)/shard_map/ppermute | solution.py:394
  32.6 5.6 %collective-permute-done.from_odd = f32[9,8,128]{2,1,0:T(8,128)S(1)} collective-permute-done((f32[9,8,128]{2,1,0:T(8,128)S(1)}, f32[9,8,128]{2,1,0:T(8,128)S(1)}, u32[]{:S(2)}, u32[]{:S(2)}) %collective-permute-start) | collective-permute-done | bytes 36896 | tf_op jit(solution)/shard_map/ppermute | solution.py:394
  38.2 0.0 collective-permute-done.1.from_even
  38.2 0.0 collective-permute-done.2.block_even.from_even
  38.3 1.9 %collective-permute-start.4 = (f32[54,8,128]{2,1,0:T(8,128)S(1)}, f32[54,8,128]{2,1,0:T(8,128)S(1)}, u32[]{:S(2)}, u32[]{:S(2)}) collective-permute-start(f32[54,8,128]{2,1,0:T(8,128)S(1)} %get-tuple-element.17.corner_own), channel_id=1, source_target_pairs={{1,2},{2,1},{3,4},{4,3},{5,6},{6,5},{7,8},{8,7},{9,10},{10,9},{11,... | collective-permute-start | bytes 663560 | tf_op jit(solution)/shard_map/ppermute | solution.py:394
  40.9 0.0 copy-start
  40.9 0.0 copy-start.1
  40.9 0.0 collective-permute-done.3.block_odd.from_odd
  40.9 1.9 %collective-permute-start.5 = (f32[22,8,128]{2,1,0:T(8,128)S(1)}, f32[22,8,128]{2,1,0:T(8,128)S(1)}, u32[]{:S(2)}, u32[]{:S(2)}) collective-permute-start(f32[22,8,128]{2,1,0:T(8,128)S(1)} %shard_map.150), channel_id=1, source_target_pairs={{0,1},{1,0},{2,3},{3,2},{4,5},{5,4},{6,7},{7,6},{8,9},{9,8},{10,11... | collective-permute-start | bytes 270344 | tf_op jit(solution)/shard_map/ppermute | solution.py:394
  42.9 0.1 fusion.4.cos_ref
  42.9 1.2 %collective-permute-done.5.corner_even = f32[22,8,128]{2,1,0:T(8,128)S(1)} collective-permute-done((f32[22,8,128]{2,1,0:T(8,128)S(1)}, f32[22,8,128]{2,1,0:T(8,128)S(1)}, u32[]{:S(2)}, u32[]{:S(2)}) %collective-permute-start.5) | collective-permute-done | bytes 90144 | tf_op jit(solution)/shard_map/ppermute | solution.py:394
  44.1 6.2 %collective-permute-done.4.corner_odd = f32[54,8,128]{2,1,0:T(8,128)S(1)} collective-permute-done((f32[54,8,128]{2,1,0:T(8,128)S(1)}, f32[54,8,128]{2,1,0:T(8,128)S(1)}, u32[]{:S(2)}, u32[]{:S(2)}) %collective-permute-start.4) | collective-permute-done | bytes 221216 | tf_op jit(solution)/shard_map/ppermute | solution.py:394
  50.3 0.0 copy-done
  50.3 0.0 copy-done.1
  50.3 7.9 %shard_map.151 = (f32[16,8,128]{2,1,0:T(8,128)}, f32[16,8,128]{2,1,0:T(8,128)}, f32[16,8,128]{2,1,0:T(8,128)}) custom-call(f32[2,16]{1,0:T(2,128)S(4)} %get-tuple-element.11.table, f32[1,256]{1,0:T(1,128)S(1)} %fusion.4.cos_ref, f32[8,128]{1,0:T(8,128)S(1)} %get-tuple-element.15.parity, f32[8,16,8,128]{3,2,1,0:T(8,128)S(1)} %get-tuple-element.14.block.own, ...), custom_call_target="tpu_custom_call" | custom-call | tf_op jit(solution)/shard_map/pallas_call | solution.py:484
  (2 shorter events, 0.1 us)
Async XLA Ops:
  2.1 36.1 %collective-permute-start.2 = (f32[8,16,8,128]{3,2,1,0:T(8,128)S(1)}, f32[8,16,8,128]{3,2,1,0:T(8,128)S(1)}, u32[]{:S(2)}, u32[]{:S(2)}) collective-permute-start(f32[8,16,8,128]{3,2,1,0:T(8,128)S(1)} %get-tuple-element.14.block.own), channel_id=1, source_target_pairs={{0,1},{1,0},{2,3},{3,2},{4,5},{5,4},{6,7},{7,6},{8,9},{9,8},{10,11... | collective-permute-start | bytes 1572872 | tf_op jit(solution)/shard_map/ppermute | solution.py:394
  4.0 36.8 %collective-permute-start.3 = (f32[6,16,8,128]{3,2,1,0:T(8,128)S(1)}, f32[6,16,8,128]{3,2,1,0:T(8,128)S(1)}, u32[]{:S(2)}, u32[]{:S(2)}) collective-permute-start(f32[6,16,8,128]{3,2,1,0:T(8,128)S(1)} %get-tuple-element.16), channel_id=1, source_target_pairs={{1,2},{2,1},{3,4},{4,3},{5,6},{6,5},{7,8},{8,7},{9,10},{10,9},{11,... | collective-permute-start | bytes 1179656 | tf_op jit(solution)/shard_map/ppermute | solution.py:394
  12.3 25.9 %collective-permute-start = (f32[9,8,128]{2,1,0:T(8,128)S(1)}, f32[9,8,128]{2,1,0:T(8,128)S(1)}, u32[]{:S(2)}, u32[]{:S(2)}) collective-permute-start(f32[9,8,128]{2,1,0:T(8,128)S(1)} %get-tuple-element.12), channel_id=1, source_target_pairs={{32,64},{64,32},{96,128},{128,96},{160,192},{192,160},{224,256},{2... | collective-permute-start | bytes 110600 | tf_op jit(solution)/shard_map/ppermute | solution.py:394
  30.7 7.5 %collective-permute-start.1 = (f32[9,8,128]{2,1,0:T(8,128)S(1)}, f32[9,8,128]{2,1,0:T(8,128)S(1)}, u32[]{:S(2)}, u32[]{:S(2)}) collective-permute-start(f32[9,8,128]{2,1,0:T(8,128)S(1)} %get-tuple-element.13), channel_id=1, source_target_pairs={{0,32},{32,0},{64,96},{96,64},{128,160},{160,128},{192,224},{224,1... | collective-permute-start | bytes 110600 | tf_op jit(solution)/shard_map/ppermute | solution.py:394
  38.3 12.0 %collective-permute-start.4 = (f32[54,8,128]{2,1,0:T(8,128)S(1)}, f32[54,8,128]{2,1,0:T(8,128)S(1)}, u32[]{:S(2)}, u32[]{:S(2)}) collective-permute-start(f32[54,8,128]{2,1,0:T(8,128)S(1)} %get-tuple-element.17.corner_own), channel_id=1, source_target_pairs={{1,2},{2,1},{3,4},{4,3},{5,6},{6,5},{7,8},{8,7},{9,10},{10,9},{11,... | collective-permute-start | bytes 663560 | tf_op jit(solution)/shard_map/ppermute | solution.py:394
  40.9 9.4 %copy-start = (f32[16,8,128]{2,1,0:T(8,128)S(1)}, f32[16,8,128]{2,1,0:T(8,128)}, u32[]{:S(2)}) copy-start(f32[16,8,128]{2,1,0:T(8,128)} %observations.1) | copy-start | bytes 196612
  40.9 9.4 %copy-start.1 = (f32[16,8,128]{2,1,0:T(8,128)S(1)}, f32[16,8,128]{2,1,0:T(8,128)}, u32[]{:S(2)}) copy-start(f32[16,8,128]{2,1,0:T(8,128)} %weight.1) | copy-start | bytes 196612
  40.9 3.2 %collective-permute-start.5 = (f32[22,8,128]{2,1,0:T(8,128)S(1)}, f32[22,8,128]{2,1,0:T(8,128)S(1)}, u32[]{:S(2)}, u32[]{:S(2)}) collective-permute-start(f32[22,8,128]{2,1,0:T(8,128)S(1)} %shard_map.150), channel_id=1, source_target_pairs={{0,1},{1,0},{2,3},{3,2},{4,5},{5,4},{6,7},{7,6},{8,9},{9,8},{10,11... | collective-permute-start | bytes 270344 | tf_op jit(solution)/shard_map/ppermute | solution.py:394
